TPU v7x, 256 devices: a 4x2x16 block of a 4x16x16 slice. The times are simulated.
256 devices in a mesh: groups: 2 (over y), fsdp: 32 (over z, core), expert: 4 (over x).
Axes of the slice: x: 4, y: 2, z: 16, core: 2. Of those that a mesh axis runs over, the one named last changes fastest.
The devices are a block of a 4x16x16 slice.
Arguments:
- queries: bfloat16 [4096, 2048], P(('groups', 'fsdp'), 'expert'), parts along dimension 0, may hold values from -14 to 14
- keys: bfloat16 [64, 2048, 512], P(('groups', 'fsdp'), None, 'expert'), parts along dimension 0, may hold values from -14 to 14
- values: bfloat16 [64, 2048, 512], P(('groups', 'fsdp'), None, 'expert'), parts along dimension 0, may hold values from -4 to 4
- out_weight: bfloat16 [2048, 4096], P('expert', 'fsdp'), may hold values from -0.5 to 0.5
- residual: bfloat16 [4096, 4096], P(('groups', 'fsdp')), parts along dimension 0, may hold values from -3 to 3
- norm_gain: float32 [4096], replicated, may hold values from 0.5 to 1.5
- route_ids: int32 [4096, 2], P(('groups', 'fsdp')), parts along dimension 0, may hold values from 0 to 7, as said below
- route_slots: int32 [4096, 2], P(('groups', 'fsdp')), parts along dimension 0, may hold values from 0 to 23, as said below
- route_weights: int32 [4096, 2], P(('groups', 'fsdp')), parts along dimension 0, may hold values from 1 to 65535, as said below
- w_gate: bfloat16 [8, 4096, 7168], P('expert', None, 'fsdp'), may hold values from -0.09375 to 0.09375
- w_up: bfloat16 [8, 4096, 7168], P('expert', None, 'fsdp'), may hold values from -0.09375 to 0.09375
- w_down: bfloat16 [8, 7168, 4096], P('expert', 'fsdp'), may hold values from -0.0625 to 0.0625
Outputs:
- layer_out: bfloat16 [4096, 4096], P(('groups', 'fsdp'), 'expert'), parts along dimension 0
There are 2 independent parts, one for each index of `groups`. A program takes and returns all parts, laid end to end along the dimension named above; an argument that names none is the same for every part. Nothing has to cross between parts.
Inputs may be any that keep to these rules, and one draw needn't show every extreme that they name: `route_ids`: each row names two different experts. Among the rows of one block, no expert is named more than 24 times and no group of experts 2 g and 2 g + 1 more than 36 times; one expert, the same for all blocks, is named exactly 24 times in every block and its group exactly 36 times; every expert is named in every block. `route_slots`: within one block, the routes to one expert hold the slots 0 to their count - 1, each once. `route_weights`: the two entries of a row sum to 65536.
All inputs are finite; a program needn't handle non-finite values.
Results may differ from a plain program's by a relative error of at most 0.02.
Values may be sent and summed in bfloat16 or wider, within the bound.
A program may use at most 128 MiB of HBM per device.

v0:
```python
import jax
import jax.numpy as jnp
from jax import lax
from jax.sharding import PartitionSpec as P

HEAD_DIM = 128
GCAP = 36


eps = 1e-05


def copy_for_each(shard, axis):
    copies = jnp.broadcast_to(shard, (lax.axis_size(axis), *shard.shape))
    return lax.all_to_all(copies, axis, split_axis=0, concat_axis=0, tiled=True)


def taken_together(shard, axis):
    everything = copy_for_each(shard, axis)
    return jnp.sum(everything.astype(jnp.float32), axis=0)


def sent_together(arrays, axis, dim, along):
    columns = [a.reshape(*a.shape[:along], -1) for a in arrays]
    both = jnp.concatenate(columns, axis=along)
    result, at, outs = (lax.all_gather(both, axis, axis=dim, tiled=True), 0, [])
    for a, column in zip(arrays, columns):
        slab = result[..., at : at + column.shape[along]]
        outs.append(slab.reshape(*slab.shape[:along], *a.shape[along:]))
        at += column.shape[along]
    return tuple(outs)


def in_blocks(shard, dim, peers):
    before, after = (shard.shape[:dim], shard.shape[dim + 1 :])
    return jnp.moveaxis(shard.reshape(*before, peers, -1, *after), dim, 0)


def summed_on_arrival(shard, axis, dim):
    peers = lax.axis_size(axis)
    pieces = lax.all_to_all(in_blocks(shard, dim, peers), axis, 0, 0, tiled=True)
    return jnp.sum(pieces.astype(jnp.float32), axis=0)


def attend(queries, keys, values):
    block = queries.shape[0]
    context = keys.shape[1]
    kv_dev = keys.shape[2] // HEAD_DIM
    heads_dev = queries.shape[1] // HEAD_DIM
    group = heads_dev // kv_dev
    query_heads = queries.reshape(block, kv_dev, group, HEAD_DIM)
    key_heads = keys[0].reshape(context, kv_dev, HEAD_DIM)
    value_heads = values[0].reshape(context, kv_dev, HEAD_DIM)
    scores = jnp.einsum(
        "qcgd,kcd->cgqk", query_heads, key_heads, preferred_element_type=jnp.float32
    ) * HEAD_DIM ** (-0.5)
    key_pos = jnp.arange(context)
    query_pos = context - block + jnp.arange(block)
    allowed = key_pos[None, :] <= query_pos[:, None]
    masked = jnp.where(allowed, scores, -1e30)
    highest = jnp.max(masked, axis=-1, keepdims=True)
    weights = jnp.where(allowed, jnp.exp(masked - highest), 0.0)
    probs = (weights / jnp.sum(weights, axis=-1, keepdims=True)).astype(jnp.bfloat16)
    heads_out = jnp.einsum("cgqk,kcd->qcgd", probs, value_heads, preferred_element_type=jnp.float32)
    return heads_out.astype(jnp.bfloat16).reshape(block, heads_dev * HEAD_DIM)


def per_device(
    queries,
    keys,
    values,
    out_weight,
    residual,
    norm_gain,
    route_ids,
    route_slots,
    route_weights,
    w_gate,
    w_up,
    w_down,
):
    heads_out = attend(queries, keys, values)
    partial_attn = jnp.dot(
        heads_out,
        lax.all_gather(out_weight, "fsdp", axis=1, tiled=True),
        preferred_element_type=jnp.float32,
    )
    attn = taken_together(partial_attn.astype(jnp.bfloat16), "expert").astype(jnp.float32)
    hstate = (residual.astype(jnp.float32) + attn).astype(jnp.bfloat16)
    state = hstate.astype(jnp.float32)
    scale = lax.rsqrt(jnp.mean(state * state, axis=-1, keepdims=True) + eps)
    normed = (state * scale * norm_gain).astype(jnp.bfloat16)
    group_index = lax.axis_index("expert")
    first_expert = 2 * group_index
    within = route_ids - first_expert
    in_group = (within >= 0) & (within < 2)
    lead_count = jnp.sum((route_ids == first_expert).astype(jnp.int32))
    target = jnp.where(in_group, route_slots + within * lead_count, -1)
    row_ids = jnp.arange(GCAP)
    one_hot = (
        (target[None, :, 0] == row_ids[:, None]) | (target[None, :, 1] == row_ids[:, None])
    ).astype(jnp.bfloat16)
    dispatch = jnp.dot(one_hot, normed, preferred_element_type=jnp.float32).astype(jnp.bfloat16)
    second = (row_ids >= lead_count).astype(jnp.bfloat16)
    rows, labels = sent_together((dispatch, second), "fsdp", 0, 1)
    gate = jnp.einsum("nd,edf->enf", rows, w_gate, preferred_element_type=jnp.float32)
    upper = jnp.einsum("nd,edf->enf", rows, w_up, preferred_element_type=jnp.float32)
    labels_f = labels.astype(jnp.float32)
    keep = jnp.stack([1.0 - labels_f, labels_f], axis=0)[:, :, None]
    values_new = (jax.nn.silu(gate) * upper * keep).astype(jnp.bfloat16)
    flat_out = lax.psum_scatter(
        jnp.einsum("enf,efd->nd", values_new, w_down, preferred_element_type=jnp.float32).astype(
            jnp.bfloat16
        ),
        "fsdp",
        scatter_dimension=0,
        tiled=True,
    ).astype(jnp.float32)
    row_index = route_slots + within * lead_count
    safe_index = jnp.where(in_group, row_index, 0)
    shares = jnp.where(in_group, route_weights.astype(jnp.float32) / 65536.0, 0.0)
    picked = jnp.take(flat_out, safe_index, axis=0)
    contrib = jnp.sum(shares[:, :, None] * picked, axis=1)
    moe = summed_on_arrival(contrib.astype(jnp.bfloat16), "expert", 1)
    width = moe.shape[1]
    own_state = lax.dynamic_slice_in_dim(hstate, group_index * width, width, 1)
    return (own_state.astype(jnp.float32) + moe).astype(jnp.bfloat16)


def solution(mesh):
    in_specs = (
        P(("groups", "fsdp"), "expert"),
        P(("groups", "fsdp"), None, "expert"),
        P(("groups", "fsdp"), None, "expert"),
        P("expert", "fsdp"),
        P(("groups", "fsdp"), None),
        P(),
        P(("groups", "fsdp"), None),
        P(("groups", "fsdp"), None),
        P(("groups", "fsdp"), None),
        P("expert", None, "fsdp"),
        P("expert", None, "fsdp"),
        P("expert", "fsdp", None),
    )
    out_specs = P(("groups", "fsdp"), "expert")
    return jax.shard_map(
        per_device, mesh=mesh, in_specs=in_specs, out_specs=out_specs, check_vma=False
    )
```

profile of v0, /device:TPU:33, one launch (start us, length us, event | category | flops | bytes accessed | tf_op | source)
XLA Modules:
  0.0 378.2 jit_solution(10625348687652536732)
XLA Ops:
  7.6 1.5 fusion.33
  10.4 92.5 %all-gather.4.cloned.1.call-done = bf16[512,4096]{1,0:T(8,128)(2,1)} async-done(((bf16[512,128]{1,0:T(8,128)(2,1)}), bf16[512,4096]{1,0:T(8,128)(2,1)}) %all-gather.4.cloned.1.call-update) | async-done | bytes 4194320 | tf_op jit(solution)/shard_map/all_gather | solution.py:85
  102.9 3.0 convolution_convert_fusion
  105.9 1.6 broadcast_in_dim.51
  107.5 4.1 %all-to-all-start = ((bf16[4,64,4096]{2,1,0:T(8,128)(2,1)}), bf16[4,64,4096]{2,1,0:T(8,128)(2,1)S(1)}, u32[]{:S(2)}, u32[]{:S(2)}) async-start(bf16[4,64,4096]{2,1,0:T(8,128)(2,1)} %broadcast_in_dim.51), calls=%async_computation | async-start | bytes 4194304 | tf_op jit(solution)/shard_map/all_to_all | solution.py:15
  113.7 23.8 %all-to-all-done = bf16[4,64,4096]{2,1,0:T(8,128)(2,1)S(1)} async-done(((bf16[4,64,4096]{2,1,0:T(8,128)(2,1)}), bf16[4,64,4096]{2,1,0:T(8,128)(2,1)S(1)}, u32[]{:S(2)}, u32[]{:S(2)}) %all-to-all-start) | async-done | bytes 2097184 | tf_op jit(solution)/shard_map/all_to_all | solution.py:15
  139.3 75.7 %all-gather.6.cloned.1.call-done = bf16[32,36,4097]{2,1,0:T(8,128)(2,1)} async-done(((bf16[1,36,4097]{2,1,0:T(8,128)(2,1)}), bf16[32,36,4097]{2,1,0:T(8,128)(2,1)}) %all-gather.6.cloned.1.call-update) | async-done | bytes 9439504 | tf_op jit(solution)/shard_map/all_gather | solution.py:26
  215.0 14.2 %reshape.107 = bf16[1152,4097]{1,0:T(8,128)(2,1)} reshape(bf16[32,36,4097]{2,1,0:T(8,128)(2,1)} %all-gather.6.cloned.1.call-done) | data formatting | bytes 18878976
  230.4 9.8 %fusion.3 = f32[1152,448]{0,1:S(1)} fusion(bf16[4096,448]{0,1:T(8,128)(2,1)} %bitcast.70, bf16[1152,4097]{1,0:T(8,128)(2,1)} %reshape.107), kind=kOutput, calls=%fused_computation.4 | convolution fusion | flops 4227858432 | bytes 15171584
  240.2 4.9 %fusion.1 = f32[1152,448]{0,1:S(1)} fusion(bf16[4096,448]{0,1:T(8,128)(2,1)S(1)} %bitcast.71, bf16[1152,4097]{1,0:T(8,128)(2,1)S(1)} %copy-done.2), kind=kOutput, calls=%fused_computation.2 | convolution fusion | flops 4227858432 | bytes 15171584
  245.2 7.6 %bitcast_convert_fusion = bf16[1152,4096]{1,0:T(8,128)(2,1)} fusion(bf16[2,224,4096]{2,1,0:T(8,128)(2,1)S(1)} %copy-done.10, f32[2,1152,224]{1,2,0:T(8,128)S(1)} %bitcast.73, f32[2,1152,224]{1,2,0:T(8,128)S(1)} %bitcast.72, f32[2,1152]{1,0:T(2,128)S(1)} %pad_maximum_fusion), kind=kOutput, calls=%fused_computation.1 | convolution fusion | flops 4236189696 | bytes 17245184 | tf_op jit(solution)/shard_map/enf,efd->nd/dot_general | solution.py:112
  252.8 71.8 %fusion = bf16[40,4096]{1,0:T(8,128)(2,1)S(1)} fusion(bf16[1152,4096]{1,0:T(8,128)(2,1)} %bitcast_convert_fusion), kind=kCustom, calls=%all-reduce-scatter | all-reduce-scatter fusion | flops 5242881 | bytes 9765888
  324.7 2.5 collective-permute-start
  327.1 1.3 collective-permute-start.1
  328.5 5.9 %collective-permute-start.2 = (bf16[40,4096]{1,0:T(8,128)(2,1)S(1)}, bf16[40,4096]{1,0:T(8,128)(2,1)S(1)}, u32[]{:S(2)}, u32[]{:S(2)}) collective-permute-start(bf16[40,4096]{1,0:T(8,128)(2,1)S(1)} %fusion), channel_id=1, source_target_pairs={{0,12},{4,16},{8,20},{12,24},{16,28},{20,32},{24,36},{28,40},{32,4... | collective-permute-start | bytes 983048
  335.3 4.9 %collective-permute-start.3 = (bf16[4,4096]{1,0:T(4,128)(2,1)S(1)}, bf16[4,4096]{1,0:T(4,128)(2,1)S(1)}, u32[]{:S(2)}, u32[]{:S(2)}) collective-permute-start(bf16[4,4096]{1,0:T(4,128)(2,1)S(1)} %slice.20), channel_id=1, source_target_pairs={{0,16},{4,20},{8,24},{12,28},{16,32},{20,36},{24,40},{28,44},{32,4... | collective-permute-start | bytes 98312
  341.7 3.8 collective-permute-done.3
  345.5 1.7 concatenate.4
  347.2 1.3 gather_fusion
  348.6 2.3 reshape.97
  350.9 5.3 %multiply_reduce_fusion = bf16[64,4096]{1,0:T(8,128)(2,1)S(1)} fusion(f32[64,2,4096]{2,1,0:T(2,128)} %reshape.97, pred[64,2]{1,0:T(8,128)(4,1)S(1)} %copy.36, f32[64,2]{1,0:T(8,128)S(1)} %copy.35), kind=kLoop, calls=%fused_computation.12 | loop fusion | flops 1310720 | bytes 2622080 | tf_op jit(solution)/shard_map/reduce_sum | solution.py:123
  357.5 4.0 %all-to-all-start.1 = ((bf16[4,64,1024]{2,1,0:T(8,128)(2,1)}), bf16[4,64,1024]{2,1,0:T(8,128)(2,1)S(1)}, u32[]{:S(2)}, u32[]{:S(2)}) async-start(bf16[4,64,1024]{2,1,0:T(8,128)(2,1)} %copy.38), calls=%async_computation.1 | async-start | bytes 1048576 | tf_op jit(solution)/shard_map/all_to_all | solution.py:41
  361.5 8.2 %all-to-all-done.1 = bf16[4,64,1024]{2,1,0:T(8,128)(2,1)S(1)} async-done(((bf16[4,64,1024]{2,1,0:T(8,128)(2,1)}), bf16[4,64,1024]{2,1,0:T(8,128)(2,1)S(1)}, u32[]{:S(2)}, u32[]{:S(2)}) %all-to-all-start.1) | async-done | bytes 524320 | tf_op jit(solution)/shard_map/all_to_all | solution.py:41
  369.7 1.6 add_convert_fusion.1
  (64 shorter events, 10.5 us)
Async XLA Ops:
  6.5 1.0 copy-start
  6.6 96.4 %all-gather.4.cloned.1.call-start = ((), (), s32[]{:S(2)}) async-start(), calls=%async_computation.2 | async-start | bytes 4325376 | tf_op jit(solution)/shard_map/all_gather | solution.py:85
  7.6 2.0 copy-start.11
  107.5 4.2 %copy-start.5 = (s32[64,2]{0,1:T(2,128)S(1)}, s32[64,2]{0,1:T(2,128)}, u32[]{:S(2)}) copy-start(s32[64,2]{0,1:T(2,128)} %param.18) | copy-start | bytes 1540
  107.5 5.5 %copy-start.7 = (s32[64,2]{0,1:T(2,128)S(1)}, s32[64,2]{0,1:T(2,128)}, u32[]{:S(2)}) copy-start(s32[64,2]{0,1:T(2,128)} %param.20) | copy-start | bytes 1540
  107.5 5.5 %copy-start.6 = (s32[64,2]{0,1:T(2,128)S(1)}, s32[64,2]{0,1:T(2,128)}, u32[]{:S(2)}) copy-start(s32[64,2]{0,1:T(2,128)} %param.19) | copy-start | bytes 1540
  107.5 30.0 %all-to-all-start = ((bf16[4,64,4096]{2,1,0:T(8,128)(2,1)}), bf16[4,64,4096]{2,1,0:T(8,128)(2,1)S(1)}, u32[]{:S(2)}, u32[]{:S(2)}) async-start(bf16[4,64,4096]{2,1,0:T(8,128)(2,1)} %broadcast_in_dim.51), calls=%async_computation | async-start | bytes 4194304 | tf_op jit(solution)/shard_map/all_to_all | solution.py:15
  111.7 26.2 %copy-start.4 = (bf16[64,4096]{1,0:T(8,128)(2,1)S(1)}, bf16[64,4096]{1,0:T(8,128)(2,1)}, u32[]{:S(2)}) copy-start(bf16[64,4096]{1,0:T(8,128)(2,1)} %param.16) | copy-start | bytes 1572868
  111.7 103.3 %all-gather.6.cloned.1.call-start = ((), (), s32[]{:S(2)}) async-start(), calls=%async_computation.3 | async-start | bytes 11151360 | tf_op jit(solution)/shard_map/all_gather | solution.py:26
  113.7 24.5 %copy-start.12 = (f32[4096]{0:T(1024)S(1)}, f32[4096]{0:T(1024)}, u32[]{:S(2)}) copy-start(f32[4096]{0:T(1024)} %param.17) | copy-start | bytes 49156
  138.1 91.1 %copy-start.3 = (bf16[64,4096]{1,0:T(8,128)(2,1)}, bf16[64,4096]{1,0:T(8,128)(2,1)S(1)}, u32[]{:S(2)}) copy-start(bf16[64,4096]{1,0:T(8,128)(2,1)S(1)} %get-tuple-element.10) | copy-start | bytes 1572868
  230.4 9.8 %copy-start.2 = (bf16[1152,4097]{1,0:T(8,128)(2,1)S(1)}, bf16[1152,4097]{1,0:T(8,128)(2,1)}, u32[]{:S(2)}) copy-start(bf16[1152,4097]{1,0:T(8,128)(2,1)} %reshape.107) | copy-start | bytes 28318468
  230.4 9.8 %copy-start.9 = (bf16[2,4096,224]{1,2,0:T(8,128)(2,1)S(1)}, bf16[2,4096,224]{1,2,0:T(8,128)(2,1)}, u32[]{:S(2)}) copy-start(bf16[2,4096,224]{1,2,0:T(8,128)(2,1)} %param.22) | copy-start | bytes 11010052
  240.2 5.0 %copy-start.10 = (bf16[2,224,4096]{2,1,0:T(8,128)(2,1)S(1)}, bf16[2,224,4096]{2,1,0:T(8,128)(2,1)}, u32[]{:S(2)}) copy-start(bf16[2,224,4096]{2,1,0:T(8,128)(2,1)} %param.23) | copy-start | bytes 11010052
  252.8 87.6 %copy-start.8 = (u32[256]{0:T(256)S(1)}, u32[256]{0:T(256)}, u32[]{:S(2)}) copy-start(u32[256]{0:T(256)} %constant.60) | copy-start | bytes 3076
  324.7 20.8 %collective-permute-start = (bf16[40,4096]{1,0:T(8,128)(2,1)S(1)}, bf16[40,4096]{1,0:T(8,128)(2,1)S(1)}, u32[]{:S(2)}, u32[]{:S(2)}) collective-permute-start(bf16[40,4096]{1,0:T(8,128)(2,1)S(1)} %fusion), channel_id=1, source_target_pairs={{0,4},{4,8},{8,12},{12,16},{16,20},{20,24},{24,28},{28,32},{32,36}... | collective-permute-start | bytes 983048
  327.1 18.3 %collective-permute-start.1 = (bf16[40,4096]{1,0:T(8,128)(2,1)S(1)}, bf16[40,4096]{1,0:T(8,128)(2,1)S(1)}, u32[]{:S(2)}, u32[]{:S(2)}) collective-permute-start(bf16[40,4096]{1,0:T(8,128)(2,1)S(1)} %fusion), channel_id=1, source_target_pairs={{0,8},{4,12},{8,16},{12,20},{16,24},{20,28},{24,32},{28,36},{32,40... | collective-permute-start | bytes 983048
  328.5 17.0 %collective-permute-start.2 = (bf16[40,4096]{1,0:T(8,128)(2,1)S(1)}, bf16[40,4096]{1,0:T(8,128)(2,1)S(1)}, u32[]{:S(2)}, u32[]{:S(2)}) collective-permute-start(bf16[40,4096]{1,0:T(8,128)(2,1)S(1)} %fusion), channel_id=1, source_target_pairs={{0,12},{4,16},{8,20},{12,24},{16,28},{20,32},{24,36},{28,40},{32,4... | collective-permute-start | bytes 983048
  335.3 10.2 %collective-permute-start.3 = (bf16[4,4096]{1,0:T(4,128)(2,1)S(1)}, bf16[4,4096]{1,0:T(4,128)(2,1)S(1)}, u32[]{:S(2)}, u32[]{:S(2)}) collective-permute-start(bf16[4,4096]{1,0:T(4,128)(2,1)S(1)} %slice.20), channel_id=1, source_target_pairs={{0,16},{4,20},{8,24},{12,28},{16,32},{20,36},{24,40},{28,44},{32,4... | collective-permute-start | bytes 98312
  350.9 20.5 %copy-start.1 = (bf16[1,2048,128]{2,1,0:T(8,128)(2,1)S(1)}, bf16[1,2048,128]{2,1,0:T(8,128)(2,1)}, u32[]{:S(2)}) copy-start(bf16[1,2048,128]{2,1,0:T(8,128)(2,1)} %param.13) | copy-start | bytes 1572868
  357.5 12.2 %all-to-all-start.1 = ((bf16[4,64,1024]{2,1,0:T(8,128)(2,1)}), bf16[4,64,1024]{2,1,0:T(8,128)(2,1)S(1)}, u32[]{:S(2)}, u32[]{:S(2)}) async-start(bf16[4,64,1024]{2,1,0:T(8,128)(2,1)} %copy.38), calls=%async_computation.1 | async-start | bytes 1048576 | tf_op jit(solution)/shard_map/all_to_all | solution.py:41
Sparse Core Ops, SparseCore 0:
  9.1 93.7 all-gather.3
  139.5 75.4 all-gather.5
where the time goes:
time: 384 us; the launch traced here: 378 us
  waiting for transfers between devices  205 us (53%)
  blocking collectives  71.8 us (19%)
  matrix products  27.9 us (7%)
  local copies, waits for them, and re-layouts  23.7 us (6%)
  starting transfers between devices  22.7 us (6%)
  between operations  14.4 us (4%)
  other arithmetic  12.8 us (3%)
    all_gather x1, waiting for transfers between devices, per_device(): lax.all_gather(out_weight, 'fsdp', axis=1, tiled=True)  92.5 us
    all_gather x1, waiting for transfers between devices, sent_together(): result, at, outs = (lax.all_gather(both, axis, axis=dim, tiled=True), 0, [])  75.7 us
    unnamed x1, blocking collectives  71.8 us
    all_to_all x1, waiting for transfers between devices, copy_for_each(): return lax.all_to_all(copies, axis, split_axis=0, concat_axis=0, tiled=True)  23.8 us
    unnamed x30, local copies, waits for them, and re-layouts  16.7 us
    unnamed x2, matrix products  14.7 us
    unnamed x4, starting transfers between devices  14.6 us
    all_to_all x1, waiting for transfers between devices, summed_on_arrival(): lax.all_to_all(in_blocks(shard, dim, peers), axis, 0, 0, tiled=True)  8.2 us
  transfers between devices with their start and end apart: 8, of which 5 were waited for; matrix products, arithmetic and copies ran while one was open for 2% of the time, Pallas kernels for 0%

commit v1 on v0

v1 whole, which is shorter than its diff:
```python
import functools

import jax
import jax.numpy as jnp
from jax import lax
from jax.experimental import pallas as pl
from jax.experimental.pallas import tpu as pltpu
from jax.sharding import PartitionSpec as P

HEAD_DIM = 128
GCAP = 36
SUBS = 4
EPS = 1e-05
MESH = pl.DeviceIdType.MESH
F32 = jnp.float32
BF16 = jnp.bfloat16


def dot(a, b):
    return jnp.dot(a, b, preferred_element_type=F32)


def layer_kernel(
    nz,
    q_ref,
    k_hbm,
    v_hbm,
    ow_hbm,
    res_hbm,
    gain_ref,
    ids_ref,
    slots_ref,
    weights_ref,
    wg_hbm,
    wu_hbm,
    wd_hbm,
    out_ref,
    keys,
    vals,
    res,
    wg,
    wu,
    wd,
    heads,
    ow,
    xa,
    xar,
    xb,
    xbr,
    hst,
    own,
    oth,
    rows,
    cnt,
    acc,
    hid,
    part,
    dbuf,
    rbuf,
    fin,
    finr,
    con,
    conr,
    lsem,
    d0_s,
    d0_r,
    r1_s,
    r1_r,
    d1_s,
    d1_r,
    xa_s,
    xa_r,
    xb_s,
    xb_r,
    ot_s,
    ot_r,
    r2_s,
    r2_r,
    d2_s,
    d2_r,
    c0_s,
    c0_r,
    cr_s,
    cr_r,
    cd_s,
    cd_r,
    db_s,
    db_r,
    rs_s,
    rs_r,
    fi_s,
    fi_r,
    co_s,
    co_r,
):
    half = nz // 2
    n2 = lax.axis_index("fsdp")
    c = lax.rem(n2, 2)
    z = n2 // 2
    x = lax.axis_index("expert")
    step_dir = 2 * c - 1
    ring_next = {"fsdp": lax.rem(z + step_dir + nz, nz) * 2 + c}
    ring_prev = {"fsdp": lax.rem(z - step_dir + nz, nz) * 2 + c}
    sibling = {"fsdp": z * 2 + 1 - c}
    x_first = {"expert": x + 1 - 2 * lax.rem(x, 2)}
    x_second = {"expert": 3 - x}
    x_other = [{"expert": lax.rem(x + o, 4)} for o in range(4)]

    def unit_at(s):
        return lax.rem(z + s * step_dir + 2 * nz, nz)

    def sub_at(k):
        return lax.rem(2 * c + k, SUBS)

    def send(src, dst, s_sem, r_sem, device):
        return pltpu.make_async_remote_copy(
            src_ref=src, dst_ref=dst, send_sem=s_sem, recv_sem=r_sem,
            device_id=device, device_id_type=MESH,
        )

    def ring1(s, j, u):
        ref = ow.at[u, j]
        return send(ref, ref, r1_s.at[s, j], r1_r.at[s, j], ring_next)

    def pair1(s, j, u):
        ref = ow.at[u, j]
        return send(ref, ref, d1_s.at[s, j], d1_r.at[s, j], sibling)

    def ring2(s, j, u):
        ref = rows.at[u, j]
        return send(ref, ref, r2_s.at[s, j], r2_r.at[s, j], ring_next)

    def pair2(s, j, u):
        ref = rows.at[u, j]
        return send(ref, ref, d2_s.at[s, j], d2_r.at[s, j], sibling)

    def count_ring(s, u):
        return send(cnt.at[u], cnt.at[u], cr_s.at[s], cr_r.at[s], ring_next)

    def count_pair(s, u):
        return send(cnt.at[u], cnt.at[u], cd_s.at[s], cd_r.at[s], sibling)

    def swap_a(s):
        return send(xa.at[s], xar.at[s], xa_s.at[s], xa_r.at[s], x_first)

    def swap_b(s):
        return send(xb.at[s], xbr.at[s], xb_s.at[s], xb_r.at[s], x_second)

    def give(s, j, u):
        return send(part.at[u, j], dbuf.at[s - 1, j], db_s.at[s - 1, j], db_r.at[s - 1, j], sibling)

    def ring3(t, j, u):
        return send(part.at[u, j], rbuf.at[t - 1, j], rs_s.at[t - 1, j], rs_r.at[t - 1, j], ring_next)

    own_rows = ow_hbm.shape[0] // 2
    loads = [
        pltpu.make_async_copy(ow_hbm.at[pl.ds(0, own_rows)], ow.at[z, 2 * c], lsem.at[0]),
        pltpu.make_async_copy(ow_hbm.at[pl.ds(own_rows, own_rows)], ow.at[z, 2 * c + 1], lsem.at[1]),
        pltpu.make_async_copy(k_hbm.at[0], keys, lsem.at[2]),
        pltpu.make_async_copy(v_hbm.at[0], vals, lsem.at[3]),
        pltpu.make_async_copy(res_hbm, res, lsem.at[4]),
        pltpu.make_async_copy(wg_hbm, wg, lsem.at[5]),
        pltpu.make_async_copy(wu_hbm, wu, lsem.at[6]),
        pltpu.make_async_copy(wd_hbm, wd, lsem.at[7]),
    ]
    for load in loads:
        load.start()

    barrier = pltpu.get_barrier_semaphore()
    partners = [ring_next, ring_prev, sibling, *x_other[1:]]
    for device in partners:
        pl.semaphore_signal(barrier, inc=1, device_id=device, device_id_type=MESH)
    pl.semaphore_wait(barrier, len(partners))

    loads[0].wait()
    loads[1].wait()
    for i in range(2):
        j = 2 * c + i
        send(ow.at[z, j], ow.at[z, j], d0_s.at[i], d0_r.at[i], sibling).start()
        ring1(1, j, z).start()
    for i in range(2):
        j = 2 * (1 - c) + i
        send(ow.at[z, j], ow.at[z, j], d0_s.at[i], d0_r.at[i], sibling).wait_recv()
        ring1(1, j, z).start()

    loads[2].wait()
    loads[3].wait()
    block, heads_width = q_ref.shape
    context = keys.shape[0]
    key_pos = lax.broadcasted_iota(jnp.int32, (block, context), 1)
    query_pos = context - block + lax.broadcasted_iota(jnp.int32, (block, context), 0)
    allowed = key_pos <= query_pos
    for h in range(heads_width // HEAD_DIM):
        cols = slice(h * HEAD_DIM, (h + 1) * HEAD_DIM)
        scores = lax.dot_general(
            q_ref[:, cols], keys[...], (((1,), (1,)), ((), ())), preferred_element_type=F32
        ) * HEAD_DIM ** (-0.5)
        masked = jnp.where(allowed, scores, -1e30)
        highest = jnp.max(masked, axis=-1, keepdims=True)
        weights = jnp.where(allowed, jnp.exp(masked - highest), 0.0)
        probs = (weights / jnp.sum(weights, axis=-1, keepdims=True)).astype(BF16)
        heads[:, cols] = dot(probs, vals[...]).astype(BF16)

    unit = 2 * ow.shape[3]
    lane = ow.shape[3]

    def project(s):
        for pos, u in enumerate((unit_at(-s), unit_at(s))):
            for b in range(2):
                total = dot(heads[:, :own_rows], ow[u, 2 * b]) + dot(
                    heads[:, own_rows:], ow[u, 2 * b + 1]
                )
                at = pos * unit + b * lane
                xa[s, :, at : at + lane] = total.astype(BF16)
        swap_a(s).start()

    def add_first(s):
        swap_a(s).wait_recv()
        xb[s] = (xa[s].astype(F32) + xar[s].astype(F32)).astype(BF16)
        swap_b(s).start()

    def add_second(s):
        swap_b(s).wait_recv()
        for pos, u in enumerate((unit_at(-s), unit_at(s))):
            cols = slice(pos * unit, (pos + 1) * unit)
            attn = xb[s, :, cols].astype(F32) + xbr[s, :, cols].astype(F32)
            left = pl.ds(pl.multiple_of(u * unit, unit), unit)
            hst[u] = (res[:, left].astype(F32) + attn).astype(BF16)

    loads[4].wait()
    project(0)

    def projection_step(s, carry):
        u = unit_at(-s)
        for k in range(SUBS):
            j = sub_at(k)
            ring1(s, j, u).wait_recv()
            if k < 2:
                ring1(s + 1, j, u).start()
            else:
                @pl.when(s < half - 1)
                def _():
                    ring1(s + 1, j, u).start()
            pair1(s, j, u).start()
        for j in range(SUBS):
            pair1(s, j, unit_at(s)).wait_recv()
        project(s)
        add_first(s - 1)

        @pl.when(s >= 2)
        def _():
            add_second(s - 2)

        return carry

    lax.fori_loop(1, half, projection_step, 0)
    u = unit_at(half)
    for k in range(2):
        j = sub_at(k)
        ring1(half, j, u).wait_recv()
        pair1(half, j, u).start()
    for k in range(2, 4):
        pair1(half, sub_at(k), u).wait_recv()
    project(half)
    add_first(half - 1)
    add_second(half - 2)
    add_first(half)
    add_second(half - 1)
    add_second(half)

    width = rows.shape[3]
    per_sub = width // unit
    d_model = width * SUBS
    square = jnp.zeros((block, 1), F32)
    for i in range(nz):
        state = hst[i].astype(F32)
        square = square + jnp.sum(state * state, axis=-1, keepdims=True)
    scale = lax.rsqrt(square / d_model + EPS)
    first_expert = 2 * x
    ids = ids_ref[...]
    within = ids - first_expert
    in_group = (within >= 0) & (within < 2)
    is_first = jnp.where(ids == first_expert, 1.0, 0.0)
    lead = jnp.sum(jnp.sum(is_first, axis=1, keepdims=True), axis=0, keepdims=True)
    lead_i = lead.astype(jnp.int32)
    target = jnp.where(in_group, slots_ref[...] + within * lead_i + GCAP * c, -1)
    row_ids = lax.broadcasted_iota(jnp.int32, (block, 2 * GCAP), 1)
    picks = [(target[:, k : k + 1] == row_ids) for k in range(2)]
    one_hot = jnp.where(picks[0] | picks[1], 1.0, 0.0).astype(BF16)
    cnt[z, c] = jnp.broadcast_to(lead, cnt.shape[2:])
    to_sibling = send(cnt.at[z, c], cnt.at[z, c], c0_s.at[0], c0_r.at[0], sibling)
    to_sibling.start()
    for k in range(SUBS):
        j = sub_at(k)
        for i in range(per_sub):
            u = j * per_sub + i
            gain = gain_ref[:, pl.ds(pl.multiple_of(u * unit, unit), unit)]
            normed = (hst[u].astype(F32) * scale * gain).astype(BF16)
            own[j, :, i * unit : (i + 1) * unit] = lax.dot_general(
                one_hot, normed, (((0,), (0,)), ((), ())), preferred_element_type=F32
            ).astype(BF16)
        send(own.at[j], oth.at[j], ot_s.at[j], ot_r.at[j], sibling).start()
    send(cnt.at[z, 1 - c], cnt.at[z, 1 - c], c0_s.at[0], c0_r.at[0], sibling).wait_recv()
    count_ring(1, z).start()
    for k in range(SUBS):
        j = sub_at(k)
        send(own.at[j], oth.at[j], ot_s.at[j], ot_r.at[j], sibling).wait_recv()
        rows[z, j] = own[j] + oth[j]
        ring2(1, j, z).start()

    for load in loads[5:]:
        load.wait()
    unit_rows = 2 * GCAP
    ffw = wg.shape[2]

    def arrive_count(s, last):
        u = unit_at(-s)
        count_ring(s, u).wait_recv()
        if not last:
            count_ring(s + 1, u).start()
            count_pair(s, u).start()

    def gate_up(s, k, places):
        j = sub_at(k)
        slab = pl.ds(pl.multiple_of(j * width, width), width)
        for pos, u in places:
            block_rows = rows[u, j]
            for e in range(2):
                g = dot(block_rows, wg[e, slab, :])
                up = dot(block_rows, wu[e, slab, :])
                if k == 0:
                    acc[pos, e] = g
                    acc[pos, 2 + e] = up
                else:
                    acc[pos, e] += g
                    acc[pos, 2 + e] += up

    def activate(s, places):
        row = lax.broadcasted_iota(jnp.int32, (unit_rows, ffw), 0).astype(F32)
        upper = row >= GCAP
        place = jnp.where(upper, row - GCAP, row)
        for pos, u in places:
            limit = jnp.where(upper, cnt[u, 1, 0:1, 0:1], cnt[u, 0, 0:1, 0:1])
            second = place >= limit
            for e in range(2):
                g, up = acc[pos, e], acc[pos, 2 + e]
                value = g / (1.0 + jnp.exp(-g)) * up
                mine = second if e == 1 else jnp.logical_not(second)
                hid[lax.rem(s, 2), pos, e] = jnp.where(mine, value, 0.0).astype(BF16)

    def down(s, k, places):
        j = sub_at(k)
        cols = pl.ds(pl.multiple_of(j * width, width), width)
        for pos, u in places:
            total = dot(hid[lax.rem(s, 2), pos, 0], wd[0, :, cols])
            total = total + dot(hid[lax.rem(s, 2), pos, 1], wd[1, :, cols])
            part[u, j] = total.astype(BF16)

    def both(s):
        return ((0, unit_at(-s)), (1, unit_at(s)))

    def expert_step(s, carry):
        arrive_count(s, False)
        u = unit_at(-s)
        for k in range(SUBS):
            j = sub_at(k)
            ring2(s, j, u).wait_recv()
            if k < 2:
                ring2(s + 1, j, u).start()
            else:
                @pl.when(s < half - 1)
                def _():
                    ring2(s + 1, j, u).start()
            pair2(s, j, u).start()

            @pl.when(s >= 2)
            def _():
                pair2(s - 1, j, unit_at(s - 1)).wait_recv()

            gate_up(s - 1, k, both(s - 1))
            if k == SUBS - 1:
                @pl.when(s >= 2)
                def _():
                    count_pair(s - 1, unit_at(s - 1)).wait_recv()

                activate(s - 1, both(s - 1))

            @pl.when(s >= 2)
            def _():
                down(s - 2, k, both(s - 2))

            @pl.when(s >= 3)
            def _():
                give(s - 2, j, unit_at(2 - s)).start()

        return carry

    lax.fori_loop(1, half, expert_step, 0)

    far = unit_at(half)
    arrive_count(half, True)
    for k in range(SUBS):
        j = sub_at(k)
        if k < 2:
            ring2(half, j, far).wait_recv()
            pair2(half, j, far).start()
        pair2(half - 1, j, unit_at(half - 1)).wait_recv()
        gate_up(half - 1, k, both(half - 1))
        down(half - 2, k, both(half - 2))
        if half - 2 >= 1:
            give(half - 2, j, unit_at(2 - half)).start()
    count_pair(half - 1, unit_at(half - 1)).wait_recv()
    activate(half - 1, both(half - 1))
    single = ((0, far),)
    for k in range(SUBS):
        if k >= 2:
            pair2(half, sub_at(k), far).wait_recv()
        gate_up(half, k, single)
    activate(half, single)
    for k in (2, 3, 0, 1):
        down(half, k, single)
        if k >= 2:
            give(half, sub_at(k), far).start()

    for k in range(2):
        j = sub_at(k)
        give(half, j, far).wait_recv()
        part[far, j] = (part[far, j].astype(F32) + dbuf[half - 1, j].astype(F32)).astype(BF16)
        ring3(1, j, far).start()
    for k in range(SUBS):
        j = sub_at(k)
        down(half - 1, k, both(half - 1))
        give(half - 1, j, unit_at(1 - half)).start()

    def sum_sub(t, k, arrived):
        j = sub_at(k)
        u = unit_at(half - t)
        give(half - t, j, u).wait_recv()
        total = part[u, j].astype(F32) + dbuf[half - t - 1, j].astype(F32)
        if arrived:
            ring3(t, j, u).wait_recv()
            total = total + rbuf[t - 1, j].astype(F32)
        part[u, j] = total.astype(BF16)
        ring3(t + 1, j, u).start()

    for k in (2, 3, 0, 1):
        sum_sub(1, k, k < 2)

    def sum_step(t, carry):
        for k in range(SUBS):
            sum_sub(t, (k + 2) % SUBS, True)
        return carry

    lax.fori_loop(2, half, sum_step, 0)

    def finish(j):
        return send(fin.at[j], finr.at[j], fi_s.at[j], fi_r.at[j], sibling)

    for k in (2, 3, 0, 1):
        j = sub_at(k)
        ring3(half, j, z).wait_recv()
        fin[j] = (part[z, j].astype(F32) + rbuf[half - 1, j].astype(F32)).astype(BF16)
        finish(j).start()

    share = jnp.where(in_group, weights_ref[...].astype(F32) / 65536.0, 0.0)
    chosen = [jnp.where(pick, 1.0, 0.0).astype(BF16) for pick in picks]

    def combine(j):
        finish(j).wait_recv()
        total = (fin[j].astype(F32) + finr[j].astype(F32)).astype(BF16)
        return share[:, 0:1] * dot(chosen[0], total) + share[:, 1:2] * dot(chosen[1], total)

    def deliver(o):
        return send(con.at[o - 1], conr.at[o - 1], co_s.at[o - 1], co_r.at[o - 1], x_other[o])

    for o in (2, 1, 3):
        con[o - 1] = combine(lax.rem(x + o, 4)).astype(BF16)
        deliver(o).start()
    mine = combine(x)
    for i in range(per_sub):
        cols = slice(i * unit, (i + 1) * unit)
        out_ref[:, cols] = hst[x * per_sub + i].astype(BF16)
    for o in (1, 3, 2):
        deliver(o).wait_recv()
    moe = mine + conr[0].astype(F32) + conr[1].astype(F32) + conr[2].astype(F32)
    out_ref[...] = (out_ref[...].astype(F32) + moe).astype(BF16)

    for i in range(2):
        send(ow.at[z, i], ow.at[z, i], d0_s.at[i], d0_r.at[i], sibling).wait_send()
    to_sibling.wait_send()

    def drain(s, carry):
        count_ring(s, z).wait_send()
        swap_a(s - 1).wait_send()
        swap_b(s - 1).wait_send()
        for j in range(SUBS):
            @pl.when(s < half)
            def _():
                for make in (ring1, ring2, pair1, pair2, give):
                    make(s, j, z).wait_send()
                ring3(s + 1, j, z).wait_send()

        @pl.when(s < half)
        def _():
            count_pair(s, z).wait_send()

        return carry

    lax.fori_loop(1, half + 1, drain, 0)
    swap_a(half).wait_send()
    swap_b(half).wait_send()
    for k in range(2):
        j = sub_at(k)
        for make in (ring1, ring2, pair1, pair2):
            make(half, j, z).wait_send()
        give(half, sub_at(k + 2), z).wait_send()
        ring3(1, j, z).wait_send()
    for j in range(SUBS):
        send(own.at[j], oth.at[j], ot_s.at[j], ot_r.at[j], sibling).wait_send()
        finish(j).wait_send()
    for o in (1, 2, 3):
        deliver(o).wait_send()


def per_device(nz, *args):
    (queries, keys, values, out_weight, residual, gain, ids, slots, weights, w_gate, w_up, w_down) = args
    block, heads_width = queries.shape
    d_model = residual.shape[1]
    width = d_model // SUBS
    half = nz // 2
    lane = out_weight.shape[1]
    ow_rows = out_weight.shape[0] // 2
    unit_rows = 2 * GCAP
    ffw = w_gate.shape[2]
    vmem = pl.BlockSpec(memory_space=pltpu.VMEM)
    hbm = pl.BlockSpec(memory_space=pl.ANY)
    dma = pltpu.SemaphoreType.DMA
    swap = pltpu.VMEM((half + 1, block, 4 * lane), BF16)
    sub = pltpu.VMEM((SUBS, unit_rows, width), BF16)
    scratch = [
        pltpu.VMEM(keys.shape[1:], BF16),
        pltpu.VMEM(values.shape[1:], BF16),
        pltpu.VMEM(residual.shape, BF16),
        pltpu.VMEM(w_gate.shape, BF16),
        pltpu.VMEM(w_up.shape, BF16),
        pltpu.VMEM(w_down.shape, BF16),
        pltpu.VMEM((block, heads_width), BF16),
        pltpu.VMEM((nz, SUBS, ow_rows, lane), BF16),
        swap,
        swap,
        swap,
        swap,
        pltpu.VMEM((nz, block, 2 * lane), BF16),
        sub,
        sub,
        pltpu.VMEM((nz, SUBS, unit_rows, width), BF16),
        pltpu.VMEM((nz, 2, 8, 128), F32),
        pltpu.VMEM((2, 4, unit_rows, ffw), F32),
        pltpu.VMEM((2, 2, 2, unit_rows, ffw), BF16),
        pltpu.VMEM((nz, SUBS, unit_rows, width), BF16),
        pltpu.VMEM((half, SUBS, unit_rows, width), BF16),
        pltpu.VMEM((half, SUBS, unit_rows, width), BF16),
        sub,
        sub,
        pltpu.VMEM((3, block, width), BF16),
        pltpu.VMEM((3, block, width), BF16),
        dma((8,)),
        dma((2,)),
        dma((2,)),
        *[dma((half + 1, SUBS))] * 4,
        *[dma((half + 1,))] * 4,
        *[dma((SUBS,))] * 2,
        *[dma((half + 1, SUBS))] * 4,
        *[dma((1,))] * 2,
        *[dma((half + 1,))] * 4,
        *[dma((half, SUBS))] * 4,
        *[dma((SUBS,))] * 2,
        *[dma((3,))] * 2,
    ]
    return pl.pallas_call(
        functools.partial(layer_kernel, nz),
        out_shape=jax.ShapeDtypeStruct((block, width), BF16),
        in_specs=[vmem, hbm, hbm, hbm, hbm, vmem, vmem, vmem, vmem, hbm, hbm, hbm],
        out_specs=vmem,
        scratch_shapes=scratch,
        compiler_params=pltpu.CompilerParams(
            collective_id=0, has_side_effects=True, vmem_limit_bytes=67043328
        ),
    )(queries, keys, values, out_weight, residual, gain.reshape(1, -1), ids, slots, weights, w_gate, w_up, w_down)


def solution(mesh):
    in_specs = (
        P(("groups", "fsdp"), "expert"),
        P(("groups", "fsdp"), None, "expert"),
        P(("groups", "fsdp"), None, "expert"),
        P("expert", "fsdp"),
        P(("groups", "fsdp"), None),
        P(),
        P(("groups", "fsdp"), None),
        P(("groups", "fsdp"), None),
        P(("groups", "fsdp"), None),
        P("expert", None, "fsdp"),
        P("expert", None, "fsdp"),
        P("expert", "fsdp", None),
    )
    return jax.shard_map(
        functools.partial(per_device, mesh.shape["fsdp"] // 2),
        mesh=mesh,
        in_specs=in_specs,
        out_specs=P(("groups", "fsdp"), "expert"),
        check_vma=False,
    )
```

time: 384 us -> 205 us (0.53); the launches traced: 378 us -> 204 us
  waiting for transfers between devices: 205 us -> 0 us
  Pallas kernels: 0 us -> 186 us
  blocking collectives: 71.8 us -> 0 us
  matrix products: 27.9 us -> 0 us
  starting transfers between devices: 22.7 us -> 0 us
  between operations: 14.4 us -> 0.01 us
  other arithmetic: 12.8 us -> 0 us
  local copies, waits for them, and re-layouts: 23.7 us -> 18.1 us
    pallas_call x0 -> x1, Pallas kernels: none -> 186 us  [per_device(): pl.pallas_call(functools.partial(layer_kernel, nz), out_shape=jax.ShapeDt...]
    all_gather x2 -> x0, waiting for transfers between devices: 168 us -> none  [the longest x1 92.5 us: per_device(): lax.all_gather(out_weight, 'fsdp', axis=1, tiled=True)]
    unnamed x1 -> x0, blocking collectives: 71.8 us -> none
    all_to_all x2 -> x0, waiting for transfers between devices: 32 us -> none  [the longest x1 23.8 us: copy_for_each(): return lax.all_to_all(copies, axis, split_axis=0, concat_axis=0, tiled=True)]
    unnamed x2 -> x0, matrix products: 14.7 us -> none
    unnamed x4 -> x0, starting transfers between devices: 14.6 us -> none
    dot_general x5 -> x0, matrix products: 13.2 us -> none  [the longest x1 7.64 us: per_device(): jnp.einsum('enf,efd->nd', values_new, w_down, preferred_element_type=jnp....]
    all_to_all x2 -> x0, starting transfers between devices: 8.13 us -> none  [the longest x1 4.12 us: copy_for_each(): return lax.all_to_all(copies, axis, split_axis=0, concat_axis=0, tiled=True)]
  transfers between devices with their start and end apart: 8 -> 0, of which waited for: 5 -> 0; matrix products, arithmetic and copies ran while one was open for 2% -> 0% of each run, Pallas kernels for 0% -> 0%
where the time goes in v1:
time: 205 us; the launch traced here: 204 us
  Pallas kernels  186 us (91%)
  local copies, waits for them, and re-layouts  18.1 us (9%)
    pallas_call x1, Pallas kernels, per_device(): pl.pallas_call(functools.partial(layer_kernel, nz), out_shape=jax.ShapeDt...  186 us
    unnamed x6, local copies, waits for them, and re-layouts  18.1 us

profile of v1, /device:TPU:33, one launch (start us, length us, event | category | flops | bytes accessed | tf_op | source)
XLA Modules:
  0.0 204.1 jit_solution(11479142172667904624)
XLA Ops:
  0.0 1.4 copy.13.ids_ref
  1.4 1.4 copy.14.slots_ref
  2.7 1.4 copy.15.weights_ref
  4.1 6.2 %copy.16.wg_hbm = bf16[2,4096,224]{2,1,0:T(8,128)(2,1)} copy(bf16[2,4096,224]{1,2,0:T(8,128)(2,1)} %param.21) | data formatting | bytes 7340032 | tf_op args[9]
  10.3 6.2 %copy.17.wu_hbm = bf16[2,4096,224]{2,1,0:T(8,128)(2,1)} copy(bf16[2,4096,224]{1,2,0:T(8,128)(2,1)} %param.22) | data formatting | bytes 7340032 | tf_op args[10]
  16.6 185.9 %shard_map.118 = bf16[64,1024]{1,0:T(8,128)(2,1)} custom-call(bf16[64,512]{1,0:T(8,128)(2,1)} %q_ref.1, bf16[1,2048,128]{2,1,0:T(8,128)(2,1)} %k_hbm.1, bf16[1,2048,128]{2,1,0:T(8,128)(2,1)} %v_hbm.1, bf16[512,128]{1,0:T(8,128)(2,1)} %ow_hbm.1, bf16[64,4096]{1,0:T(8,128)(2,1)} %res_hbm.1, f32[1,4096]{1,0:T(1,128)} %bitcast.1, s32[64,2]{1,0:T(8,128)} %copy.13.ids_ref, ...), custom_call_target="tpu_custom_call" | custom-call | tf_op jit(solution)/shard_map/pallas_call | solution.py:580
  202.5 1.6 copy.19

commit v2 on v1

--- a/solution.py
+++ b/solution.py
@@ -61,6 +61,10 @@
     finr,
     con,
     conr,
+    own_out,
+    xh,
+    xhr,
+    mix,
     lsem,
     d0_s,
     d0_r,
@@ -92,6 +96,8 @@
     fi_r,
     co_s,
     co_r,
+    xh_s,
+    xh_r,
 ):
     half = nz // 2
     n2 = lax.axis_index("fsdp")
@@ -228,7 +234,10 @@
             hst[u] = (res[:, left].astype(F32) + attn).astype(BF16)
 
     loads[4].wait()
-    project(0)
+
+    def take_pair(s):
+        for j in range(SUBS):
+            pair1(s, j, unit_at(s)).wait_recv()
 
     def projection_step(s, carry):
         u = unit_at(-s)
@@ -242,32 +251,53 @@
                 def _():
                     ring1(s + 1, j, u).start()
             pair1(s, j, u).start()
-        for j in range(SUBS):
-            pair1(s, j, unit_at(s)).wait_recv()
-        project(s)
-        add_first(s - 1)
-
         @pl.when(s >= 2)
         def _():
-            add_second(s - 2)
+            take_pair(s - 1)
+
+        project(s - 1)
+        @pl.when(s >= 2)
+        def _():
+            add_first(s - 2)
+
+        @pl.when(s >= 3)
+        def _():
+            add_second(s - 3)
 
         return carry
 
     lax.fori_loop(1, half, projection_step, 0)
     u = unit_at(half)
-    for k in range(2):
-        j = sub_at(k)
-        ring1(half, j, u).wait_recv()
-        pair1(half, j, u).start()
+    ring1(half, sub_at(0), u).wait_recv()
+    pair1(half, sub_at(0), u).start()
+    take_pair(half - 1)
+    project(half - 1)
+    ring1(half, sub_at(1), u).wait_recv()
+    pair1(half, sub_at(1), u).start()
+    add_first(half - 2)
+    if half >= 3:
+        add_second(half - 3)
     for k in range(2, 4):
         pair1(half, sub_at(k), u).wait_recv()
-    project(half)
+    for b in range(2):
+        total = dot(heads[:, :own_rows], ow[u, 2 * b]) + dot(heads[:, own_rows:], ow[u, 2 * b + 1])
+        xh[:, b * lane : (b + 1) * lane] = total.astype(BF16)
+
+    def spread(o):
+        return send(xh, xhr.at[o - 1], xh_s.at[o - 1], xh_r.at[o - 1], x_other[o])
+
+    for o in (2, 1, 3):
+        spread(o).start()
     add_first(half - 1)
     add_second(half - 2)
-    add_first(half)
     add_second(half - 1)
-    add_second(half)
-
+    for o in (1, 3, 2):
+        spread(o).wait_recv()
+    near = 2 - 2 * lax.rem(x, 2)
+    first = xh[...].astype(F32) + xhr[near].astype(F32)
+    attn = first + (xhr[1].astype(F32) + xhr[2 - near].astype(F32))
+    left = pl.ds(pl.multiple_of(u * unit, unit), unit)
+    hst[u] = (res[:, left].astype(F32) + attn).astype(BF16)
     width = rows.shape[3]
     per_sub = width // unit
     d_model = width * SUBS
@@ -282,11 +312,23 @@
     in_group = (within >= 0) & (within < 2)
     is_first = jnp.where(ids == first_expert, 1.0, 0.0)
     lead = jnp.sum(jnp.sum(is_first, axis=1, keepdims=True), axis=0, keepdims=True)
-    lead_i = lead.astype(jnp.int32)
-    target = jnp.where(in_group, slots_ref[...] + within * lead_i + GCAP * c, -1)
-    row_ids = lax.broadcasted_iota(jnp.int32, (block, 2 * GCAP), 1)
-    picks = [(target[:, k : k + 1] == row_ids) for k in range(2)]
+    target = jnp.where(in_group, slots_ref[...] + within * lead.astype(jnp.int32) + GCAP * c, -1)
+    row_ids = lax.broadcasted_iota(jnp.int32, (2 * GCAP, block), 0)
+    picks = [row_ids == target[k : k + 1, :] for k in range(2)]
     one_hot = jnp.where(picks[0] | picks[1], 1.0, 0.0).astype(BF16)
+    share = weights_ref[...].astype(F32) / 65536.0
+    mixed = jnp.where(picks[0], share[0:1, :], 0.0) + jnp.where(picks[1], share[1:2, :], 0.0)
+    high = mixed.astype(BF16)
+    low = (mixed - high.astype(F32)).astype(BF16)
+    same = (
+        lax.broadcasted_iota(jnp.int32, (block, block), 0)
+        == lax.broadcasted_iota(jnp.int32, (block, block), 1)
+    )
+    turn = jnp.where(same, 1.0, 0.0).astype(BF16)
+    for i, piece in enumerate((high, low)):
+        mix[i] = lax.dot_general(
+            turn, piece, (((1,), (1,)), ((), ())), preferred_element_type=F32
+        ).astype(BF16)
     cnt[z, c] = jnp.broadcast_to(lead, cnt.shape[2:])
     to_sibling = send(cnt.at[z, c], cnt.at[z, c], c0_s.at[0], c0_r.at[0], sibling)
     to_sibling.start()
@@ -296,9 +338,7 @@
             u = j * per_sub + i
             gain = gain_ref[:, pl.ds(pl.multiple_of(u * unit, unit), unit)]
             normed = (hst[u].astype(F32) * scale * gain).astype(BF16)
-            own[j, :, i * unit : (i + 1) * unit] = lax.dot_general(
-                one_hot, normed, (((0,), (0,)), ((), ())), preferred_element_type=F32
-            ).astype(BF16)
+            own[j, :, i * unit : (i + 1) * unit] = dot(one_hot, normed).astype(BF16)
         send(own.at[j], oth.at[j], ot_s.at[j], ot_r.at[j], sibling).start()
     send(cnt.at[z, 1 - c], cnt.at[z, 1 - c], c0_s.at[0], c0_r.at[0], sibling).wait_recv()
     count_ring(1, z).start()
@@ -311,7 +351,8 @@
     for load in loads[5:]:
         load.wait()
     unit_rows = 2 * GCAP
-    ffw = wg.shape[2]
+    ffw = wg.shape[1]
+    quarter = width // SUBS
 
     def arrive_count(s, last):
         u = unit_at(-s)
@@ -320,44 +361,53 @@
             count_ring(s + 1, u).start()
             count_pair(s, u).start()
 
-    def gate_up(s, k, places):
+    def gate_up(k, units):
         j = sub_at(k)
         slab = pl.ds(pl.multiple_of(j * width, width), width)
-        for pos, u in places:
-            block_rows = rows[u, j]
-            for e in range(2):
-                g = dot(block_rows, wg[e, slab, :])
-                up = dot(block_rows, wu[e, slab, :])
-                if k == 0:
-                    acc[pos, e] = g
-                    acc[pos, 2 + e] = up
-                else:
-                    acc[pos, e] += g
-                    acc[pos, 2 + e] += up
-
-    def activate(s, places):
-        row = lax.broadcasted_iota(jnp.int32, (unit_rows, ffw), 0).astype(F32)
-        upper = row >= GCAP
-        place = jnp.where(upper, row - GCAP, row)
-        for pos, u in places:
-            limit = jnp.where(upper, cnt[u, 1, 0:1, 0:1], cnt[u, 0, 0:1, 0:1])
-            second = place >= limit
-            for e in range(2):
-                g, up = acc[pos, e], acc[pos, 2 + e]
-                value = g / (1.0 + jnp.exp(-g)) * up
-                mine = second if e == 1 else jnp.logical_not(second)
-                hid[lax.rem(s, 2), pos, e] = jnp.where(mine, value, 0.0).astype(BF16)
-
-    def down(s, k, places):
+        block_rows = jnp.concatenate([rows[u, j] for u in units], axis=0)
+        many = len(units) * unit_rows
+        for i in range(4):
+            weight = (wg, wu)[i // 2]
+            total = lax.dot_general(
+                block_rows, weight[i % 2, :, slab], (((1,), (1,)), ((), ())),
+                preferred_element_type=F32,
+            )
+            if k == 0:
+                acc[i, :many] = total
+            else:
+                acc[i, :many] += total
+
+    def activate(slot, units):
+        many = len(units) * unit_rows
+        row = lax.broadcasted_iota(jnp.int32, (many, ffw), 0).astype(F32)
+        limit = cnt[units[0], 0, 0:1, 0:1]
+        start = jnp.zeros((1, 1), F32)
+        place = row
+        for i in range(1, 2 * len(units)):
+            later = row >= i * GCAP
+            limit = jnp.where(later, cnt[units[i // 2], i % 2, 0:1, 0:1], limit)
+            place = jnp.where(later, row - i * GCAP, place)
+        second = place >= limit
+        for e in range(2):
+            g, up = acc[e, :many], acc[2 + e, :many]
+            value = g / (1.0 + jnp.exp(-g)) * up
+            mine = second if e == 1 else jnp.logical_not(second)
+            hid[slot, e, :many] = jnp.where(mine, value, 0.0).astype(BF16)
+
+    def down(slot, k, units):
         j = sub_at(k)
-        cols = pl.ds(pl.multiple_of(j * width, width), width)
-        for pos, u in places:
-            total = dot(hid[lax.rem(s, 2), pos, 0], wd[0, :, cols])
-            total = total + dot(hid[lax.rem(s, 2), pos, 1], wd[1, :, cols])
-            part[u, j] = total.astype(BF16)
+        many = len(units) * unit_rows
+        for f in range(SUBS):
+            start = f * width + j * quarter
+            cols = pl.ds(pl.multiple_of(start, quarter), quarter)
+            total = dot(hid[slot, 0, :many], wd[0, :, cols]) + dot(hid[slot, 1, :many], wd[1, :, cols])
+            for i, u in enumerate(units):
+                part[u, j, :, f * quarter : (f + 1) * quarter] = total[
+                    i * unit_rows : (i + 1) * unit_rows
+                ].astype(BF16)
 
     def both(s):
-        return ((0, unit_at(-s)), (1, unit_at(s)))
+        return (unit_at(-s), unit_at(s))
 
     def expert_step(s, carry):
         arrive_count(s, False)
@@ -377,17 +427,17 @@
             def _():
                 pair2(s - 1, j, unit_at(s - 1)).wait_recv()
 
-            gate_up(s - 1, k, both(s - 1))
+            gate_up(k, both(s - 1))
             if k == SUBS - 1:
                 @pl.when(s >= 2)
                 def _():
                     count_pair(s - 1, unit_at(s - 1)).wait_recv()
 
-                activate(s - 1, both(s - 1))
+                activate(lax.rem(s - 1, 3), both(s - 1))
 
             @pl.when(s >= 2)
             def _():
-                down(s - 2, k, both(s - 2))
+                down(lax.rem(s - 2, 3), k, both(s - 2))
 
             @pl.when(s >= 3)
             def _():
@@ -400,37 +450,18 @@
     far = unit_at(half)
     arrive_count(half, True)
     for k in range(SUBS):
-        j = sub_at(k)
-        if k < 2:
-            ring2(half, j, far).wait_recv()
-            pair2(half, j, far).start()
-        pair2(half - 1, j, unit_at(half - 1)).wait_recv()
-        gate_up(half - 1, k, both(half - 1))
-        down(half - 2, k, both(half - 2))
-        if half - 2 >= 1:
-            give(half - 2, j, unit_at(2 - half)).start()
+        pair2(half - 1, sub_at(k), unit_at(half - 1)).wait_recv()
+        if k == SUBS - 1:
+            ring2(half, sub_at(0), far).wait_recv()
+            pair2(half, sub_at(0), far).start()
+        gate_up(k, both(half - 1))
     count_pair(half - 1, unit_at(half - 1)).wait_recv()
-    activate(half - 1, both(half - 1))
-    single = ((0, far),)
+    activate((half - 1) % 3, both(half - 1))
     for k in range(SUBS):
-        if k >= 2:
-            pair2(half, sub_at(k), far).wait_recv()
-        gate_up(half, k, single)
-    activate(half, single)
-    for k in (2, 3, 0, 1):
-        down(half, k, single)
-        if k >= 2:
-            give(half, sub_at(k), far).start()
-
-    for k in range(2):
-        j = sub_at(k)
-        give(half, j, far).wait_recv()
-        part[far, j] = (part[far, j].astype(F32) + dbuf[half - 1, j].astype(F32)).astype(BF16)
-        ring3(1, j, far).start()
-    for k in range(SUBS):
-        j = sub_at(k)
-        down(half - 1, k, both(half - 1))
-        give(half - 1, j, unit_at(1 - half)).start()
+        down((half - 1) % 3, k, both(half - 1))
+        give(half - 1, sub_at(k), unit_at(1 - half)).start()
+    ring2(half, sub_at(1), far).wait_recv()
+    pair2(half, sub_at(1), far).start()
 
     def sum_sub(t, k, arrived):
         j = sub_at(k)
@@ -443,48 +474,78 @@
         part[u, j] = total.astype(BF16)
         ring3(t + 1, j, u).start()
 
+    sum_sub(1, 2, False)
+    sum_sub(1, 3, False)
+    single = (far,)
+    for k in range(SUBS):
+        if k >= 2:
+            pair2(half, sub_at(k), far).wait_recv()
+        gate_up(k, single)
+    activate(half % 3, single)
     for k in (2, 3, 0, 1):
-        sum_sub(1, k, k < 2)
+        down(half % 3, k, single)
+        if k >= 2:
+            give(half, sub_at(k), far).start()
+    sum_sub(0, 0, False)
+    sum_sub(0, 1, False)
+    for k in range(SUBS):
+        down((half - 2) % 3, k, both(half - 2))
+        if half > 2:
+            give(half - 2, sub_at(k), unit_at(2 - half)).start()
 
     def sum_step(t, carry):
-        for k in range(SUBS):
-            sum_sub(t, (k + 2) % SUBS, True)
+        sum_sub(t + 1, 2, True)
+        sum_sub(t + 1, 3, True)
+        sum_sub(t, 0, True)
+        sum_sub(t, 1, True)
         return carry
 
-    lax.fori_loop(2, half, sum_step, 0)
+    lax.fori_loop(1, half - 1, sum_step, 0)
+    sum_sub(half - 1, 0, True)
+    sum_sub(half - 1, 1, True)
 
     def finish(j):
         return send(fin.at[j], finr.at[j], fi_s.at[j], fi_r.at[j], sibling)
 
-    for k in (2, 3, 0, 1):
+    def close(k):
         j = sub_at(k)
         ring3(half, j, z).wait_recv()
         fin[j] = (part[z, j].astype(F32) + rbuf[half - 1, j].astype(F32)).astype(BF16)
         finish(j).start()
 
-    share = jnp.where(in_group, weights_ref[...].astype(F32) / 65536.0, 0.0)
-    chosen = [jnp.where(pick, 1.0, 0.0).astype(BF16) for pick in picks]
+    def deliver(j, o):
+        at = SUBS * (o - 1) + j
+        return send(con.at[at], conr.at[at], co_s.at[at], co_r.at[at], x_other[o])
 
     def combine(j):
         finish(j).wait_recv()
-        total = (fin[j].astype(F32) + finr[j].astype(F32)).astype(BF16)
-        return share[:, 0:1] * dot(chosen[0], total) + share[:, 1:2] * dot(chosen[1], total)
-
-    def deliver(o):
-        return send(con.at[o - 1], conr.at[o - 1], co_s.at[o - 1], co_r.at[o - 1], x_other[o])
-
-    for o in (2, 1, 3):
-        con[o - 1] = combine(lax.rem(x + o, 4)).astype(BF16)
-        deliver(o).start()
-    mine = combine(x)
-    for i in range(per_sub):
-        cols = slice(i * unit, (i + 1) * unit)
-        out_ref[:, cols] = hst[x * per_sub + i].astype(BF16)
-    for o in (1, 3, 2):
-        deliver(o).wait_recv()
-    moe = mine + conr[0].astype(F32) + conr[1].astype(F32) + conr[2].astype(F32)
-    out_ref[...] = (out_ref[...].astype(F32) + moe).astype(BF16)
-
+        for o in (2, 1, 3, 0):
+            f = lax.rem(x + o, 4)
+            cols = pl.ds(pl.multiple_of(f * quarter, quarter), quarter)
+            total = (fin[j, :, cols].astype(F32) + finr[j, :, cols].astype(F32)).astype(BF16)
+            moe = dot(mix[0], total) + dot(mix[1], total)
+            if o:
+                con[SUBS * (o - 1) + j] = moe.astype(BF16)
+                deliver(j, o).start()
+            else:
+                at = j * quarter
+                state = hst[x * per_sub + at // unit][:, at % unit : at % unit + quarter]
+                own_out[:, at : at + quarter] = state.astype(F32) + moe
+
+    close(2)
+    close(3)
+    close(0)
+    combine(0)
+    combine(2)
+    close(1)
+    combine(1)
+    combine(3)
+    for j in (0, 2, 1, 3):
+        total = own_out[:, j * quarter : (j + 1) * quarter]
+        for o in (1, 3, 2):
+            deliver(j, o).wait_recv()
+            total = total + conr[SUBS * (o - 1) + j].astype(F32)
+        out_ref[:, j * quarter : (j + 1) * quarter] = total.astype(BF16)
     for i in range(2):
         send(ow.at[z, i], ow.at[z, i], d0_s.at[i], d0_r.at[i], sibling).wait_send()
     to_sibling.wait_send()
@@ -507,8 +568,6 @@
         return carry
 
     lax.fori_loop(1, half + 1, drain, 0)
-    swap_a(half).wait_send()
-    swap_b(half).wait_send()
     for k in range(2):
         j = sub_at(k)
         for make in (ring1, ring2, pair1, pair2):
@@ -519,7 +578,9 @@
         send(own.at[j], oth.at[j], ot_s.at[j], ot_r.at[j], sibling).wait_send()
         finish(j).wait_send()
     for o in (1, 2, 3):
-        deliver(o).wait_send()
+        spread(o).wait_send()
+        for j in range(SUBS):
+            deliver(j, o).wait_send()
 
 
 def per_device(nz, *args):
@@ -532,10 +593,12 @@
     ow_rows = out_weight.shape[0] // 2
     unit_rows = 2 * GCAP
     ffw = w_gate.shape[2]
+    quarter = width // SUBS
+    w_gate, w_up = (jnp.swapaxes(w, 1, 2) for w in (w_gate, w_up))
     vmem = pl.BlockSpec(memory_space=pltpu.VMEM)
     hbm = pl.BlockSpec(memory_space=pl.ANY)
     dma = pltpu.SemaphoreType.DMA
-    swap = pltpu.VMEM((half + 1, block, 4 * lane), BF16)
+    swap = pltpu.VMEM((half, block, 4 * lane), BF16)
     sub = pltpu.VMEM((SUBS, unit_rows, width), BF16)
     scratch = [
         pltpu.VMEM(keys.shape[1:], BF16),
@@ -555,26 +618,31 @@
         sub,
         pltpu.VMEM((nz, SUBS, unit_rows, width), BF16),
         pltpu.VMEM((nz, 2, 8, 128), F32),
-        pltpu.VMEM((2, 4, unit_rows, ffw), F32),
-        pltpu.VMEM((2, 2, 2, unit_rows, ffw), BF16),
+        pltpu.VMEM((4, 2 * unit_rows, ffw), F32),
+        pltpu.VMEM((3, 2, 2 * unit_rows, ffw), BF16),
         pltpu.VMEM((nz, SUBS, unit_rows, width), BF16),
         pltpu.VMEM((half, SUBS, unit_rows, width), BF16),
         pltpu.VMEM((half, SUBS, unit_rows, width), BF16),
         sub,
         sub,
-        pltpu.VMEM((3, block, width), BF16),
-        pltpu.VMEM((3, block, width), BF16),
+        pltpu.VMEM((3 * SUBS, block, quarter), BF16),
+        pltpu.VMEM((3 * SUBS, block, quarter), BF16),
+        pltpu.VMEM((block, width), F32),
+        pltpu.VMEM((block, 2 * lane), BF16),
+        pltpu.VMEM((3, block, 2 * lane), BF16),
+        pltpu.VMEM((2, block, unit_rows), BF16),
         dma((8,)),
         dma((2,)),
         dma((2,)),
         *[dma((half + 1, SUBS))] * 4,
-        *[dma((half + 1,))] * 4,
+        *[dma((half,))] * 4,
         *[dma((SUBS,))] * 2,
         *[dma((half + 1, SUBS))] * 4,
         *[dma((1,))] * 2,
         *[dma((half + 1,))] * 4,
         *[dma((half, SUBS))] * 4,
         *[dma((SUBS,))] * 2,
+        *[dma((3 * SUBS,))] * 2,
         *[dma((3,))] * 2,
     ]
     return pl.pallas_call(
@@ -586,7 +654,7 @@
         compiler_params=pltpu.CompilerParams(
             collective_id=0, has_side_effects=True, vmem_limit_bytes=67043328
         ),
-    )(queries, keys, values, out_weight, residual, gain.reshape(1, -1), ids, slots, weights, w_gate, w_up, w_down)
+    )(queries, keys, values, out_weight, residual, gain.reshape(1, -1), ids.T, slots.T, weights.T, w_gate, w_up, w_down)
 
 
 def solution(mesh):

time: 205 us -> 180 us (0.88)
  local copies, waits for them, and re-layouts: 18.1 us -> 1.57 us
  Pallas kernels: 186 us -> 179 us
    unnamed x6 -> x1, local copies, waits for them, and re-layouts: 18.1 us -> 1.57 us
    pallas_call x1, Pallas kernels: 186 us -> 179 us  [per_device(): pl.pallas_call(functools.partial(layer_kernel, nz), out_shape=jax.ShapeDt...]
where the time goes in v2:
time: 180 us
  Pallas kernels  179 us (99%)
    pallas_call x1, Pallas kernels, per_device(): pl.pallas_call(functools.partial(layer_kernel, nz), out_shape=jax.ShapeDt...  179 us

profile of v2, /device:TPU:33, one launch (start us, length us, event | category | flops | bytes accessed | tf_op | source)
XLA Modules:
  0.0 180.3 jit_solution(3637831263545795155)
XLA Ops:
  0.0 178.7 %shard_map.118 = bf16[64,1024]{1,0:T(8,128)(2,1)} custom-call(bf16[64,512]{1,0:T(8,128)(2,1)} %q_ref.1, bf16[1,2048,128]{2,1,0:T(8,128)(2,1)} %k_hbm.1, bf16[1,2048,128]{2,1,0:T(8,128)(2,1)} %v_hbm.1, bf16[512,128]{1,0:T(8,128)(2,1)} %ow_hbm.1, bf16[64,4096]{1,0:T(8,128)(2,1)} %res_hbm.1, f32[1,4096]{1,0:T(1,128)} %bitcast.8, s32[2,64]{1,0:T(2,128)} %bitcast.9, ...), custom_call_target="tpu_custom_call" | custom-call | tf_op jit(solution)/shard_map/pallas_call | solution.py:648
  178.7 1.6 copy.14

commit v3 on v2

v3 whole, which is shorter than its diff:
```python
import functools

import jax
import jax.numpy as jnp
from jax import lax
from jax.experimental import pallas as pl
from jax.experimental.pallas import tpu as pltpu
from jax.sharding import PartitionSpec as P

HEAD_DIM = 128
GCAP = 36
SUBS = 4
EPS = 1e-05
MESH = pl.DeviceIdType.MESH
F32 = jnp.float32
BF16 = jnp.bfloat16


def dot(a, b):
    return jnp.dot(a, b, preferred_element_type=F32)


def layer_kernel(
    nz,
    q_ref,
    k_hbm,
    v_hbm,
    ow_hbm,
    res_hbm,
    gain_ref,
    ids_ref,
    slots_ref,
    weights_ref,
    wg_hbm,
    wu_hbm,
    wd_hbm,
    out_ref,
    keys,
    vals,
    res,
    wg,
    wu,
    wd,
    heads,
    ow,
    xa,
    xar,
    xb,
    xbr,
    hst,
    own,
    oth,
    rows,
    cnt,
    acc,
    hid,
    part,
    dbuf,
    xin,
    pos,
    posr,
    zsr,
    base,
    finp,
    finpr,
    finz,
    finzr,
    con,
    conr,
    xh,
    xhr,
    mix,
    lsem,
    d0_s,
    d0_r,
    r1_s,
    r1_r,
    d1_s,
    d1_r,
    xa_s,
    xa_r,
    xb_s,
    xb_r,
    ot_s,
    ot_r,
    r2_s,
    r2_r,
    d2_s,
    d2_r,
    c0_s,
    c0_r,
    cr_s,
    cr_r,
    cd_s,
    cd_r,
    db_s,
    db_r,
    xi_s,
    xi_r,
    rs_s,
    rs_r,
    fi_s,
    fi_r,
    co_s,
    co_r,
    xh_s,
    xh_r,
):
    half = nz // 2
    half_width = zsr.shape[3]
    n2 = lax.axis_index("fsdp")
    c = lax.rem(n2, 2)
    z = n2 // 2
    x = lax.axis_index("expert")
    step_dir = 2 * c - 1
    ring_next = {"fsdp": lax.rem(z + step_dir + nz, nz) * 2 + c}
    ring_prev = {"fsdp": lax.rem(z - step_dir + nz, nz) * 2 + c}
    sibling = {"fsdp": z * 2 + 1 - c}
    x_first = {"expert": x + 1 - 2 * lax.rem(x, 2)}
    x_second = {"expert": 3 - x}
    x_other = [{"expert": lax.rem(x + o, 4)} for o in range(4)]

    def unit_at(s):
        return lax.rem(z + s * step_dir + 2 * nz, nz)

    def sub_at(k):
        return lax.rem(2 * c + k, SUBS)

    def send(src, dst, s_sem, r_sem, device):
        return pltpu.make_async_remote_copy(
            src_ref=src, dst_ref=dst, send_sem=s_sem, recv_sem=r_sem,
            device_id=device, device_id_type=MESH,
        )

    def ring1(s, j, u):
        ref = ow.at[u, j]
        return send(ref, ref, r1_s.at[s, j], r1_r.at[s, j], ring_next)

    def pair1(s, j, u):
        ref = ow.at[u, j]
        return send(ref, ref, d1_s.at[s, j], d1_r.at[s, j], sibling)

    def ring2(s, j, u):
        ref = rows.at[u, j]
        return send(ref, ref, r2_s.at[s, j], r2_r.at[s, j], ring_next)

    def pair2(s, j, u):
        ref = rows.at[u, j]
        return send(ref, ref, d2_s.at[s, j], d2_r.at[s, j], sibling)

    def count_ring(s, u):
        return send(cnt.at[u], cnt.at[u], cr_s.at[s], cr_r.at[s], ring_next)

    def count_pair(s, u):
        return send(cnt.at[u], cnt.at[u], cd_s.at[s], cd_r.at[s], sibling)

    def swap_a(s):
        return send(xa.at[s], xar.at[s], xa_s.at[s], xa_r.at[s], x_first)

    def swap_b(s):
        return send(xb.at[s], xbr.at[s], xb_s.at[s], xb_r.at[s], x_second)

    def give(s, j, u):
        return send(part.at[u, j], dbuf.at[s - 1, j], db_s.at[s - 1, j], db_r.at[s - 1, j], sibling)

    def quarter_at(o):
        return lax.rem(x + o, 4)

    def lanes(h):
        return pl.ds(pl.multiple_of(h * half_width, half_width), half_width)

    def ring_p(t, b):
        sems = rs_s.at[t, b], rs_r.at[t, b]
        return send(pos.at[half - t - 1, b], posr.at[t, b], *sems, ring_next)

    def ring_z(t, h):
        sems = rs_s.at[t, 2 + h], rs_r.at[t, 2 + h]
        src = dbuf.at[half - t - 1, quarter_at(2), :, lanes(h)]
        return send(src, zsr.at[t, h], *sems, ring_next)

    def over_far(o):
        i = 1 if o == 1 else 0
        part_rows = pl.ds(pl.multiple_of(32 * c, 32), 40)
        src = dbuf.at[half - 1, quarter_at(o), part_rows]
        dst = xin.at[half, i, part_rows]
        return send(src, dst, xi_s.at[half, i], xi_r.at[half, i], x_other[o])

    def over(s, o, src):
        i = 1 if o == 1 else 0
        return send(src, xin.at[s, i], xi_s.at[s, i], xi_r.at[s, i], x_other[o])

    own_rows = ow_hbm.shape[0] // 2
    loads = [
        pltpu.make_async_copy(ow_hbm.at[pl.ds(0, own_rows)], ow.at[z, 2 * c], lsem.at[0]),
        pltpu.make_async_copy(ow_hbm.at[pl.ds(own_rows, own_rows)], ow.at[z, 2 * c + 1], lsem.at[1]),
        pltpu.make_async_copy(k_hbm.at[0], keys, lsem.at[2]),
        pltpu.make_async_copy(v_hbm.at[0], vals, lsem.at[3]),
        pltpu.make_async_copy(res_hbm, res, lsem.at[4]),
        pltpu.make_async_copy(wg_hbm, wg, lsem.at[5]),
        pltpu.make_async_copy(wu_hbm, wu, lsem.at[6]),
        pltpu.make_async_copy(wd_hbm, wd, lsem.at[7]),
    ]
    for load in loads:
        load.start()

    xin[half] = jnp.zeros(xin.shape[1:], BF16)
    barrier = pltpu.get_barrier_semaphore()
    partners = [ring_next, ring_prev, sibling, *x_other[1:]]
    for device in partners:
        pl.semaphore_signal(barrier, inc=1, device_id=device, device_id_type=MESH)
    pl.semaphore_wait(barrier, len(partners))

    loads[0].wait()
    loads[1].wait()
    for i in range(2):
        j = 2 * c + i
        send(ow.at[z, j], ow.at[z, j], d0_s.at[i], d0_r.at[i], sibling).start()
        ring1(1, j, z).start()
    for i in range(2):
        j = 2 * (1 - c) + i
        send(ow.at[z, j], ow.at[z, j], d0_s.at[i], d0_r.at[i], sibling).wait_recv()
        ring1(1, j, z).start()

    loads[2].wait()
    loads[3].wait()
    block, heads_width = q_ref.shape
    context = keys.shape[0]
    key_pos = lax.broadcasted_iota(jnp.int32, (block, context), 1)
    query_pos = context - block + lax.broadcasted_iota(jnp.int32, (block, context), 0)
    allowed = key_pos <= query_pos
    for h in range(heads_width // HEAD_DIM):
        cols = slice(h * HEAD_DIM, (h + 1) * HEAD_DIM)
        scores = lax.dot_general(
            q_ref[:, cols], keys[...], (((1,), (1,)), ((), ())), preferred_element_type=F32
        ) * HEAD_DIM ** (-0.5)
        masked = jnp.where(allowed, scores, -1e30)
        highest = jnp.max(masked, axis=-1, keepdims=True)
        weights = jnp.where(allowed, jnp.exp(masked - highest), 0.0)
        probs = (weights / jnp.sum(weights, axis=-1, keepdims=True)).astype(BF16)
        heads[:, cols] = dot(probs, vals[...]).astype(BF16)

    unit = 2 * ow.shape[3]
    lane = ow.shape[3]

    def project(s):
        for side, u in enumerate((unit_at(-s), unit_at(s))):
            for b in range(2):
                total = dot(heads[:, :own_rows], ow[u, 2 * b]) + dot(
                    heads[:, own_rows:], ow[u, 2 * b + 1]
                )
                at = side * unit + b * lane
                xa[s, :, at : at + lane] = total.astype(BF16)
        swap_a(s).start()

    def add_first(s):
        swap_a(s).wait_recv()
        xb[s] = (xa[s].astype(F32) + xar[s].astype(F32)).astype(BF16)
        swap_b(s).start()

    def add_second(s):
        swap_b(s).wait_recv()
        for side, u in enumerate((unit_at(-s), unit_at(s))):
            cols = slice(side * unit, (side + 1) * unit)
            attn = xb[s, :, cols].astype(F32) + xbr[s, :, cols].astype(F32)
            left = pl.ds(pl.multiple_of(u * unit, unit), unit)
            hst[u] = (res[:, left].astype(F32) + attn).astype(BF16)

    first_expert = 2 * x
    ids = ids_ref[...]
    within = ids - first_expert
    in_group = (within >= 0) & (within < 2)
    is_first = jnp.where(ids == first_expert, 1.0, 0.0)
    lead = jnp.sum(jnp.sum(is_first, axis=1, keepdims=True), axis=0, keepdims=True)
    target = jnp.where(in_group, slots_ref[...] + within * lead.astype(jnp.int32) + GCAP * c, -1)
    row_ids = lax.broadcasted_iota(jnp.int32, (2 * GCAP, block), 0)
    picks = [row_ids == target[k : k + 1, :] for k in range(2)]
    picked = picks[0] | picks[1]
    one_hot = jnp.where(picked, 1.0, 0.0).astype(BF16)
    share = weights_ref[...].astype(F32) / 65536.0
    share_high = share.astype(BF16).astype(F32)
    facts = [share_high[0:1], share_high[1:2], share[0:1] - share_high[0:1], share[1:2] - share_high[1:2]]
    for o in (3, 1, 0):
        other = 2 * lax.rem(x + o, 4)
        inside = (ids >= other) & (ids < other + 2)
        count = jnp.where(ids == other, 1.0, 0.0)
        count = jnp.sum(jnp.sum(count, axis=1, keepdims=True), axis=0, keepdims=True)
        place = slots_ref[...] + (ids - other) * count.astype(jnp.int32) + GCAP * c + 1
        place = jnp.where(inside, place, 0).astype(F32)
        facts = [place[0:1], place[1:2]] + facts
    shift = (block, cnt.shape[3])
    spot = lax.broadcasted_iota(jnp.int32, shift, 0) + block * c
    placed = spot == lax.broadcasted_iota(jnp.int32, shift, 1)
    same = (
        lax.broadcasted_iota(jnp.int32, (block, block), 0)
        == lax.broadcasted_iota(jnp.int32, (block, block), 1)
    )
    line = lax.broadcasted_iota(jnp.int32, cnt.shape[2:], 0)
    info = jnp.zeros(cnt.shape[2:], F32)
    for i, fact in enumerate(facts):
        column = jnp.sum(jnp.where(same, fact, 0.0), axis=1, keepdims=True)
        wide_fact = jnp.sum(jnp.where(placed, column, 0.0), axis=0, keepdims=True)
        info = jnp.where(line == i + 2, wide_fact, info)
    mixed = jnp.where(picks[0], share[0:1, :], 0.0) + jnp.where(picks[1], share[1:2, :], 0.0)
    high = mixed.astype(BF16)
    low = (mixed - high.astype(F32)).astype(BF16)
    turn = jnp.where(same, 1.0, 0.0).astype(BF16)
    for i, piece in enumerate((high, low)):
        mix[i] = lax.dot_general(
            turn, piece, (((1,), (1,)), ((), ())), preferred_element_type=F32
        ).astype(BF16)
    loads[4].wait()

    def take_pair(s):
        for j in range(SUBS):
            pair1(s, j, unit_at(s)).wait_recv()

    def projection_step(s, carry):
        u = unit_at(-s)
        for k in range(SUBS):
            j = sub_at(k)
            ring1(s, j, u).wait_recv()
            if k < 2:
                ring1(s + 1, j, u).start()
            else:
                @pl.when(s < half - 1)
                def _():
                    ring1(s + 1, j, u).start()
            pair1(s, j, u).start()
            if k == 1:
                @pl.when(s >= 2)
                def _():
                    take_pair(s - 1)

                project(s - 1)

                @pl.when(s >= 2)
                def _():
                    add_first(s - 2)

                @pl.when(s >= 3)
                def _():
                    add_second(s - 3)

        return carry

    lax.fori_loop(1, half, projection_step, 0)
    u = unit_at(half)
    ring1(half, sub_at(0), u).wait_recv()
    pair1(half, sub_at(0), u).start()
    take_pair(half - 1)
    project(half - 1)
    ring1(half, sub_at(1), u).wait_recv()
    pair1(half, sub_at(1), u).start()
    add_first(half - 2)
    if half >= 3:
        add_second(half - 3)
    width = rows.shape[3]
    per_sub = width // unit
    d_model = width * SUBS

    def rows_at(u, k):
        return lax.rem(lax.rem(u + half + 1, nz) // per_sub + 1 + k, SUBS)

    def trade(j):
        return send(own.at[j], oth.at[j], ot_s.at[j], ot_r.at[j], sibling)

    def dispatch(k):
        j = rows_at(z, k)
        for i in range(per_sub):
            u = j * per_sub + i
            gain = gain_ref[:, pl.ds(pl.multiple_of(u * unit, unit), unit)]
            scaled = (hst[u].astype(F32) * gain).astype(BF16)
            own[j, :, i * unit : (i + 1) * unit] = dot(one_hot, scaled).astype(BF16)
        trade(j).start()

    def launch(k):
        j = rows_at(z, k)
        trade(j).wait_recv()
        rows[z, j] = own[j] + oth[j]
        ring2(1, j, z).start()

    add_second(half - 2)
    far = unit_at(half)
    for k in range(2, 4):
        pair1(half, sub_at(k), far).wait_recv()
    for b in range(2):
        total = dot(heads[:, :own_rows], ow[far, 2 * b]) + dot(
            heads[:, own_rows:], ow[far, 2 * b + 1]
        )
        xh[:, b * lane : (b + 1) * lane] = total.astype(BF16)

    def spread(o):
        return send(xh, xhr.at[o - 1], xh_s.at[o - 1], xh_r.at[o - 1], x_other[o])

    for o in (2, 1, 3):
        spread(o).start()
    dispatch(0)
    dispatch(1)
    add_first(half - 1)
    launch(0)
    launch(1)
    add_second(half - 1)
    for o in (1, 3, 2):
        spread(o).wait_recv()
    near = 2 - 2 * lax.rem(x, 2)
    first = xh[...].astype(F32) + xhr[near].astype(F32)
    attn = first + (xhr[1].astype(F32) + xhr[2 - near].astype(F32))
    left = pl.ds(pl.multiple_of(far * unit, unit), unit)
    hst[far] = (res[:, left].astype(F32) + attn).astype(BF16)
    dispatch(2)
    dispatch(3)
    square = jnp.zeros((block, 1), F32)
    for i in range(nz):
        state = hst[i].astype(F32)
        square = square + jnp.sum(state * state, axis=-1, keepdims=True)
    scale = lax.rsqrt(square / d_model + EPS)
    by_position = jnp.sum(jnp.where(same, scale, 0.0), axis=0, keepdims=True)
    by_row = jnp.sum(jnp.where(picked, by_position, 0.0), axis=1, keepdims=True)
    grid = (2 * GCAP, cnt.shape[3])
    diagonal = lax.broadcasted_iota(jnp.int32, grid, 0) == lax.broadcasted_iota(jnp.int32, grid, 1)
    row_scale = jnp.sum(jnp.where(diagonal, by_row, 0.0), axis=0, keepdims=True)
    cnt[z, c] = jnp.where(line == 0, lead, jnp.where(line == 1, row_scale, info))
    to_sibling = send(cnt.at[z, c], cnt.at[z, c], c0_s.at[0], c0_r.at[0], sibling)
    to_sibling.start()
    launch(2)
    launch(3)
    send(cnt.at[z, 1 - c], cnt.at[z, 1 - c], c0_s.at[0], c0_r.at[0], sibling).wait_recv()
    count_ring(1, z).start()
    for load in loads[5:]:
        load.wait()
    unit_rows = 2 * GCAP
    ffw = wg.shape[1]
    quarter = width // SUBS

    def arrive_count(s, last):
        u = unit_at(-s)
        count_ring(s, u).wait_recv()
        if not last:
            count_ring(s + 1, u).start()
            count_pair(s, u).start()

    def gate_up(j, units, first):
        slab = pl.ds(j * width, width) if isinstance(j, int) else pl.ds(
            pl.multiple_of(j * width, width), width
        )
        block_rows = jnp.concatenate([rows[u, j] for u in units], axis=0)
        many = len(units) * unit_rows
        for i in range(4):
            weight = (wg, wu)[i // 2]
            total = lax.dot_general(
                block_rows, weight[i % 2, :, slab], (((1,), (1,)), ((), ())),
                preferred_element_type=F32,
            )
            if first:
                acc[i, :many] = total
            else:
                acc[i, :many] += total

    def activate(slot, units):
        many = len(units) * unit_rows
        row = lax.broadcasted_iota(jnp.int32, (many, ffw), 0).astype(F32)
        limit = cnt[units[0], 0, 0:1, 0:1]
        place = row
        for i in range(1, 2 * len(units)):
            later = row >= i * GCAP
            limit = jnp.where(later, cnt[units[i // 2], i % 2, 0:1, 0:1], limit)
            place = jnp.where(later, row - i * GCAP, place)
        second = place >= limit
        wide = (many, cnt.shape[3])
        at = lax.broadcasted_iota(jnp.int32, wide, 0) - lax.broadcasted_iota(jnp.int32, wide, 1)
        factor = jnp.zeros(wide, F32)
        for i, u in enumerate(units):
            row_scale = cnt[u, 0, 1:2, :] + cnt[u, 1, 1:2, :]
            factor = factor + jnp.where(at == i * unit_rows, row_scale, 0.0)
        factor = jnp.sum(factor, axis=1, keepdims=True)
        for e in range(2):
            g, up = acc[e, :many] * factor, acc[2 + e, :many] * factor
            value = g / (1.0 + jnp.exp(-g)) * up
            mine = second if e == 1 else jnp.logical_not(second)
            hid[slot, e, :many] = jnp.where(mine, value, 0.0).astype(BF16)

    def down(slot, f, units):
        many = len(units) * unit_rows
        for i in range(SUBS):
            start = f * width + i * quarter
            if not isinstance(f, int):
                start = pl.multiple_of(start, quarter)
            cols = pl.ds(start, quarter)
            total = dot(hid[slot, 0, :many], wd[0, :, cols]) + dot(hid[slot, 1, :many], wd[1, :, cols])
            for n, u in enumerate(units):
                part[u, f, :, i * quarter : (i + 1) * quarter] = total[
                    n * unit_rows : (n + 1) * unit_rows
                ].astype(BF16)

    def both(s):
        return (unit_at(-s), unit_at(s))

    def prepare(s, last=False):
        u = unit_at(s)
        for o in (1, 3, 2, 0):
            f = quarter_at(o)
            give(s, f, u).wait_recv()
            dbuf[s - 1, f] = (part[u, f].astype(F32) + dbuf[s - 1, f].astype(F32)).astype(BF16)
            if o in (1, 3):
                (over_far(o) if last else over(s, o, dbuf.at[s - 1, f])).start()

    def by_positions(s, mine, last=False):
        for o in (1, 3):
            (over_far(o) if last else over(s, o, xin.at[s, 0])).wait_recv()
        u = unit_at(s)
        facts = cnt[u, 0] + cnt[u, 1]
        row = lax.broadcasted_iota(jnp.int32, (unit_rows, cnt.shape[3]), 0).astype(F32) + 1.0
        highs, lows = [], []
        for i in range(3):
            hit = [row == facts[2 + 2 * i + k : 3 + 2 * i + k] for k in range(2)]
            for kept, at in ((highs, 8), (lows, 10)):
                kept.append(
                    jnp.where(hit[0], facts[at : at + 1], 0.0)
                    + jnp.where(hit[1], facts[at + 1 : at + 2], 0.0)
                )
        sums = jnp.concatenate([mine, xin[s, 0], xin[s, 1]], axis=0)
        total = None
        for weight in (highs, lows):
            turned = jnp.transpose(jnp.concatenate(weight, axis=0)).astype(BF16)
            term = dot(turned, sums)
            total = term if total is None else total + term
        return total

    def gather_positions(s, last=False):
        total = by_positions(s, dbuf[s - 1, x], last)
        for b in range(2):
            pos[s - 1, b] = total[b * block : (b + 1) * block].astype(BF16)

    def sum_p(t, b, arrived):
        if arrived:
            ring_p(t - 1, b).wait_recv()
            at = half - t - 1
            pos[at, b] = (pos[at, b].astype(F32) + posr[t - 1, b].astype(F32)).astype(BF16)
        ring_p(t, b).start()

    def sum_z(t, h, arrived):
        if arrived:
            ring_z(t - 1, h).wait_recv()
            at = half - t - 1
            f = quarter_at(2)
            dbuf[at, f, :, lanes(h)] = (
                dbuf[at, f, :, lanes(h)].astype(F32) + zsr[t - 1, h].astype(F32)
            ).astype(BF16)
        ring_z(t, h).start()

    def expert_step(s, carry):
        u = unit_at(-s)
        for k in range(SUBS):
            j = rows_at(u, k)
            ring2(s, j, u).wait_recv()

            @pl.when((s < half - 1) | (c == 1 if k < 2 else c == 0))
            def _():
                ring2(s + 1, j, u).start()

            pair2(s, j, u).start()
            if k == 2:
                arrive_count(s, False)
            @pl.when(s >= 2)
            def _():
                pair2(s - 1, k, unit_at(s - 1)).wait_recv()

            gate_up(k, both(s - 1), k == 0)
            if k == SUBS - 1:
                @pl.when(s >= 2)
                def _():
                    count_pair(s - 1, unit_at(s - 1)).wait_recv()

                activate(lax.rem(s - 1, 3), both(s - 1))

            @pl.when(s >= 2)
            def _():
                down(lax.rem(s - 2, 3), k, both(s - 2))

            @pl.when(s >= 3)
            def _():
                give(s - 2, k, unit_at(2 - s)).start()

        @pl.when(s == 3)
        def _():
            for o in (1, 3):
                over(0, o, part.at[z, quarter_at(o)]).start()

        @pl.when(s >= 4)
        def _():
            prepare(s - 3)

        return carry

    lax.fori_loop(1, half, expert_step, 0)

    own_far = [rows_at(far, 2 * (1 - c) + i) for i in range(2)]
    other_far = [rows_at(far, 2 * c + i) for i in range(2)]
    prepare(half - 3)
    for k in range(SUBS):
        pair2(half - 1, k, unit_at(half - 1)).wait_recv()
        if k == SUBS - 1:
            ring2(half, own_far[0], far).wait_recv()
            pair2(half, own_far[0], far).start()
        gate_up(k, both(half - 1), k == 0)
    count_pair(half - 1, unit_at(half - 1)).wait_recv()
    activate((half - 1) % 3, both(half - 1))
    for o in (1, 3, 2, 0):
        down((half - 1) % 3, quarter_at(o), both(half - 1))
        give(half - 1, quarter_at(o), unit_at(1 - half)).start()
    ring2(half, own_far[1], far).wait_recv()
    pair2(half, own_far[1], far).start()
    arrive_count(half, True)

    prepare(half - 1)
    sum_z(1, 1 - c, False)
    single = (far,)
    for i in range(2):
        gate_up(own_far[i], single, i == 0)
    for i in range(2):
        pair2(half, other_far[i], far).wait_recv()
        gate_up(other_far[i], single, False)
    activate(half % 3, single)
    for o in (1, 3, 2, 0):
        down(half % 3, quarter_at(o), single)
        give(half, quarter_at(o), far).start()
    prepare(half, True)
    sum_z(0, c, False)
    gather_positions(half - 1)
    sum_p(1, 1 - c, False)
    for o in (1, 3, 2, 0):
        down((half - 2) % 3, quarter_at(o), both(half - 2))
        give(half - 2, quarter_at(o), unit_at(2 - half)).start()
    prepare(half - 2)
    sum_z(2, 1 - c, True)
    gather_positions(half, True)
    sum_p(0, c, False)
    sum_z(1, c, True)
    total = by_positions(0, part[z, x])
    for b in range(2):
        base[b] = total[b * block : (b + 1) * block]

    def sum_step(t, carry):
        @pl.when(t < half)
        def _():
            sum_z(t, 1 - c, True)

        gather_positions(half - t + 1)
        sum_z(t - 1, c, True)
        sum_p(t - 1, 1 - c, True)
        sum_p(t - 2, c, True)
        return carry

    lax.fori_loop(3, half + 1, sum_step, 0)

    def swap_z(h):
        return send(finz.at[h], finzr.at[h], fi_s.at[h], fi_r.at[h], sibling)

    swap_p = send(finp, finpr, fi_s.at[2], fi_r.at[2], sibling)

    def close_z(h):
        ring_z(half - 1, h).wait_recv()
        own_part = part[z, quarter_at(2), :, lanes(h)]
        finz[h] = (own_part.astype(F32) + zsr[half - 1, h].astype(F32)).astype(BF16)
        swap_z(h).start()

    def deliver(h):
        return send(con.at[h], conr.at[h], co_s.at[h], co_r.at[h], x_other[2])

    def cross(h):
        swap_z(h).wait_recv()
        total = (finz[h].astype(F32) + finzr[h].astype(F32)).astype(BF16)
        con[h] = (dot(mix[0], total) + dot(mix[1], total)).astype(BF16)
        deliver(h).start()

    close_z(1 - c)
    sum_p(half - 1, c, True)
    close_z(c)
    cross(0)
    cross(1)
    ring_p(half - 1, 1 - c).wait_recv()
    finp[...] = (base[1 - c] + posr[half - 1, 1 - c].astype(F32)).astype(BF16)
    swap_p.start()
    ring_p(half - 1, c).wait_recv()
    swap_p.wait_recv()
    base[c] = base[c] + posr[half - 1, c].astype(F32) + finpr[...].astype(F32)
    for h in range(2):
        deliver(h).wait_recv()
        for i in range(half_width // min(unit, half_width)):
            step = min(unit, half_width)
            at = h * half_width + i * step
            state = hst[x * per_sub + at // unit][:, at % unit : at % unit + step]
            total = state.astype(F32) + base[c, :, at : at + step]
            total = total + conr[h, :, i * step : (i + 1) * step].astype(F32)
            out_ref[:, at : at + step] = total.astype(BF16)
    for i in range(2):
        send(ow.at[z, i], ow.at[z, i], d0_s.at[i], d0_r.at[i], sibling).wait_send()
    to_sibling.wait_send()

    def drain(s, carry):
        count_ring(s, z).wait_send()
        swap_a(s - 1).wait_send()
        swap_b(s - 1).wait_send()
        for j in range(SUBS):
            @pl.when(s < half)
            def _():
                for make in (ring1, ring2, pair1, pair2):
                    make(s, j, z).wait_send()

            give(s, j, z).wait_send()

        @pl.when(s < half)
        def _():
            for o in (1, 3):
                over(s, o, xin.at[s, 0]).wait_send()
            count_pair(s, z).wait_send()
            for b in range(2):
                ring_p(s, b).wait_send()
                ring_z(s, b).wait_send()

        return carry

    lax.fori_loop(1, half + 1, drain, 0)
    for k in range(2):
        j = sub_at(k)
        for make in (ring1, pair1):
            make(half, j, z).wait_send()
        ring2(half, rows_at(unit_at(1 - half), 2 * (1 - c) + k), z).wait_send()
        pair2(half, own_far[k], z).wait_send()
        deliver(k).wait_send()
        swap_z(k).wait_send()
        over(0, 1 + 2 * k, xin.at[0, 0]).wait_send()
        over_far(1 + 2 * k).wait_send()
    for j in range(SUBS):
        send(own.at[j], oth.at[j], ot_s.at[j], ot_r.at[j], sibling).wait_send()
    for o in (1, 2, 3):
        spread(o).wait_send()
    ring_p(0, c).wait_send()
    ring_z(0, c).wait_send()
    swap_p.wait_send()


def per_device(nz, *args):
    (queries, keys, values, out_weight, residual, gain, ids, slots, weights, w_gate, w_up, w_down) = args
    block, heads_width = queries.shape
    d_model = residual.shape[1]
    width = d_model // SUBS
    half = nz // 2
    lane = out_weight.shape[1]
    ow_rows = out_weight.shape[0] // 2
    unit_rows = 2 * GCAP
    ffw = w_gate.shape[2]
    w_gate, w_up = (jnp.swapaxes(w, 1, 2) for w in (w_gate, w_up))
    vmem = pl.BlockSpec(memory_space=pltpu.VMEM)
    hbm = pl.BlockSpec(memory_space=pl.ANY)
    dma = pltpu.SemaphoreType.DMA
    swap = pltpu.VMEM((half, block, 4 * lane), BF16)
    sub = pltpu.VMEM((SUBS, unit_rows, width), BF16)
    scratch = [
        pltpu.VMEM(keys.shape[1:], BF16),
        pltpu.VMEM(values.shape[1:], BF16),
        pltpu.VMEM(residual.shape, BF16),
        pltpu.VMEM(w_gate.shape, BF16),
        pltpu.VMEM(w_up.shape, BF16),
        pltpu.VMEM(w_down.shape, BF16),
        pltpu.VMEM((block, heads_width), BF16),
        pltpu.VMEM((nz, SUBS, ow_rows, lane), BF16),
        swap,
        swap,
        swap,
        swap,
        pltpu.VMEM((nz, block, 2 * lane), BF16),
        sub,
        sub,
        pltpu.VMEM((nz, SUBS, unit_rows, width), BF16),
        pltpu.VMEM((nz, 2, 16, 128), F32),
        pltpu.VMEM((4, 2 * unit_rows, ffw), F32),
        pltpu.VMEM((3, 2, 2 * unit_rows, ffw), BF16),
        pltpu.VMEM((nz, SUBS, unit_rows, width), BF16),
        pltpu.VMEM((half, SUBS, unit_rows, width), BF16),
        pltpu.VMEM((half + 1, 2, unit_rows, width), BF16),
        pltpu.VMEM((half, 2, block, width), BF16),
        pltpu.VMEM((half, 2, block, width), BF16),
        pltpu.VMEM((half, 2, unit_rows, width // 2), BF16),
        pltpu.VMEM((2, block, width), F32),
        *[pltpu.VMEM((block, width), BF16)] * 2,
        *[pltpu.VMEM((2, unit_rows, width // 2), BF16)] * 2,
        *[pltpu.VMEM((2, block, width // 2), BF16)] * 2,
        pltpu.VMEM((block, 2 * lane), BF16),
        pltpu.VMEM((3, block, 2 * lane), BF16),
        pltpu.VMEM((2, block, unit_rows), BF16),
        dma((8,)),
        dma((2,)),
        dma((2,)),
        *[dma((half + 1, SUBS))] * 4,
        *[dma((half,))] * 4,
        *[dma((SUBS,))] * 2,
        *[dma((half + 1, SUBS))] * 4,
        *[dma((1,))] * 2,
        *[dma((half + 1,))] * 4,
        *[dma((half, SUBS))] * 2,
        *[dma((half + 1, 2))] * 2,
        *[dma((half, SUBS))] * 2,
        *[dma((3,))] * 2,
        *[dma((2,))] * 2,
        *[dma((3,))] * 2,
    ]
    return pl.pallas_call(
        functools.partial(layer_kernel, nz),
        out_shape=jax.ShapeDtypeStruct((block, width), BF16),
        in_specs=[vmem, hbm, hbm, hbm, hbm, vmem, vmem, vmem, vmem, hbm, hbm, hbm],
        out_specs=vmem,
        scratch_shapes=scratch,
        compiler_params=pltpu.CompilerParams(
            collective_id=0, has_side_effects=True, vmem_limit_bytes=67043328
        ),
    )(queries, keys, values, out_weight, residual, gain.reshape(1, -1), ids.T, slots.T, weights.T, w_gate, w_up, w_down)


def solution(mesh):
    in_specs = (
        P(("groups", "fsdp"), "expert"),
        P(("groups", "fsdp"), None, "expert"),
        P(("groups", "fsdp"), None, "expert"),
        P("expert", "fsdp"),
        P(("groups", "fsdp"), None),
        P(),
        P(("groups", "fsdp"), None),
        P(("groups", "fsdp"), None),
        P(("groups", "fsdp"), None),
        P("expert", None, "fsdp"),
        P("expert", None, "fsdp"),
        P("expert", "fsdp", None),
    )
    return jax.shard_map(
        functools.partial(per_device, mesh.shape["fsdp"] // 2),
        mesh=mesh,
        in_specs=in_specs,
        out_specs=P(("groups", "fsdp"), "expert"),
        check_vma=False,
    )
```

time: 180 us -> 171 us (0.950)
  Pallas kernels: 179 us -> 169 us
    pallas_call x1, Pallas kernels: 179 us -> 169 us  [per_device(): pl.pallas_call(functools.partial(layer_kernel, nz), out_shape=jax.ShapeDt...]
where the time goes in v3:
time: 171 us
  Pallas kernels  169 us (99%)
    pallas_call x1, Pallas kernels, per_device(): pl.pallas_call(functools.partial(layer_kernel, nz), out_shape=jax.ShapeDt...  169 us

profile of v3, /device:TPU:33, one launch (start us, length us, event | category | flops | bytes accessed | tf_op | source)
XLA Modules:
  0.0 170.9 jit_solution(15993354875938737769)
XLA Ops:
  0.0 169.3 %shard_map.118 = bf16[64,1024]{1,0:T(8,128)(2,1)} custom-call(bf16[64,512]{1,0:T(8,128)(2,1)} %q_ref.1, bf16[1,2048,128]{2,1,0:T(8,128)(2,1)} %k_hbm.1, bf16[1,2048,128]{2,1,0:T(8,128)(2,1)} %v_hbm.1, bf16[512,128]{1,0:T(8,128)(2,1)} %ow_hbm.1, bf16[64,4096]{1,0:T(8,128)(2,1)} %res_hbm.1, f32[1,4096]{1,0:T(1,128)} %bitcast.8, s32[2,64]{1,0:T(2,128)} %bitcast.9, ...), custom_call_target="tpu_custom_call" | custom-call | tf_op jit(solution)/shard_map/pallas_call | solution.py:808
  169.3 1.6 copy.14

commit v4 on v3

--- a/solution.py
+++ b/solution.py
@@ -41,6 +41,7 @@
     wg,
     wu,
     wd,
+    stage,
     heads,
     ow,
     xa,
@@ -71,6 +72,7 @@
     xhr,
     mix,
     lsem,
+    wsem,
     d0_s,
     d0_r,
     r1_s,
@@ -196,12 +198,32 @@
         pltpu.make_async_copy(k_hbm.at[0], keys, lsem.at[2]),
         pltpu.make_async_copy(v_hbm.at[0], vals, lsem.at[3]),
         pltpu.make_async_copy(res_hbm, res, lsem.at[4]),
-        pltpu.make_async_copy(wg_hbm, wg, lsem.at[5]),
-        pltpu.make_async_copy(wu_hbm, wu, lsem.at[6]),
-        pltpu.make_async_copy(wd_hbm, wd, lsem.at[7]),
+        pltpu.make_async_copy(wd_hbm, wd, lsem.at[5]),
     ]
-    for load in loads:
+
+    slabs = 2 * SUBS
+    slab_width = stage.shape[3]
+
+    def slab_load(m, i):
+        cols = pl.ds(pl.multiple_of((i % SUBS) * slab_width, slab_width), slab_width)
+        src = (wg_hbm, wu_hbm)[m].at[i // SUBS, :, cols]
+        return pltpu.make_async_copy(src, stage.at[m, i % 2], wsem.at[m, i % 2])
+
+    def turn_slab(m, i):
+        slab_load(m, i).wait()
+        at = pl.ds(pl.multiple_of((i % SUBS) * slab_width, slab_width), slab_width)
+        (wg, wu)[m][i // SUBS, at, :] = jnp.transpose(stage[m, i % 2])
+
+        @pl.when(i + 2 < slabs)
+        def _():
+            slab_load(m, i + 2).start()
+
+    for load in loads[:5]:
         load.start()
+    for i in range(2):
+        for m in range(2):
+            slab_load(m, jnp.int32(i)).start()
+    loads[5].start()
 
     xin[half] = jnp.zeros(xin.shape[1:], BF16)
     barrier = pltpu.get_barrier_semaphore()
@@ -326,6 +348,8 @@
                 def _():
                     ring1(s + 1, j, u).start()
             pair1(s, j, u).start()
+            if k in (0, 2):
+                turn_slab(k // 2, s - 1)
             if k == 1:
                 @pl.when(s >= 2)
                 def _():
@@ -400,6 +424,9 @@
     launch(0)
     launch(1)
     add_second(half - 1)
+    for i in range(half - 1, slabs):
+        for m in range(2):
+            turn_slab(m, jnp.int32(i))
     for o in (1, 3, 2):
         spread(o).wait_recv()
     near = 2 - 2 * lax.rem(x, 2)
@@ -429,7 +456,7 @@
     for load in loads[5:]:
         load.wait()
     unit_rows = 2 * GCAP
-    ffw = wg.shape[1]
+    ffw = wg.shape[2]
     quarter = width // SUBS
 
     def arrive_count(s, last):
@@ -447,10 +474,7 @@
         many = len(units) * unit_rows
         for i in range(4):
             weight = (wg, wu)[i // 2]
-            total = lax.dot_general(
-                block_rows, weight[i % 2, :, slab], (((1,), (1,)), ((), ())),
-                preferred_element_type=F32,
-            )
+            total = dot(block_rows, weight[i % 2, slab, :])
             if first:
                 acc[i, :many] = total
             else:
@@ -645,10 +669,10 @@
         def _():
             sum_z(t, 1 - c, True)
 
+        sum_z(t - 1, c, True)
+        sum_p(t - 2, c, True)
         gather_positions(half - t + 1)
-        sum_z(t - 1, c, True)
         sum_p(t - 1, 1 - c, True)
-        sum_p(t - 2, c, True)
         return carry
 
     lax.fori_loop(3, half + 1, sum_step, 0)
@@ -674,10 +698,10 @@
         deliver(h).start()
 
     close_z(1 - c)
-    sum_p(half - 1, c, True)
     close_z(c)
     cross(0)
     cross(1)
+    sum_p(half - 1, c, True)
     ring_p(half - 1, 1 - c).wait_recv()
     finp[...] = (base[1 - c] + posr[half - 1, 1 - c].astype(F32)).astype(BF16)
     swap_p.start()
@@ -760,9 +784,10 @@
         pltpu.VMEM(keys.shape[1:], BF16),
         pltpu.VMEM(values.shape[1:], BF16),
         pltpu.VMEM(residual.shape, BF16),
-        pltpu.VMEM(w_gate.shape, BF16),
-        pltpu.VMEM(w_up.shape, BF16),
+        pltpu.VMEM((2, d_model, ffw), BF16),
+        pltpu.VMEM((2, d_model, ffw), BF16),
         pltpu.VMEM(w_down.shape, BF16),
+        pltpu.VMEM((2, 2, ffw, width), BF16),
         pltpu.VMEM((block, heads_width), BF16),
         pltpu.VMEM((nz, SUBS, ow_rows, lane), BF16),
         swap,
@@ -789,7 +814,8 @@
         pltpu.VMEM((block, 2 * lane), BF16),
         pltpu.VMEM((3, block, 2 * lane), BF16),
         pltpu.VMEM((2, block, unit_rows), BF16),
-        dma((8,)),
+        dma((6,)),
+        dma((2, 2)),
         dma((2,)),
         dma((2,)),
         *[dma((half + 1, SUBS))] * 4,

time: 171 us -> 166 us (0.971)
  Pallas kernels: 169 us -> 165 us
    pallas_call x1, Pallas kernels: 169 us -> 165 us  [per_device(): pl.pallas_call(functools.partial(layer_kernel, nz), out_shape=jax.ShapeDt...]
where the time goes in v4:
time: 166 us
  Pallas kernels  165 us (99%)
    pallas_call x1, Pallas kernels, per_device(): pl.pallas_call(functools.partial(layer_kernel, nz), out_shape=jax.ShapeDt...  165 us

profile of v4, /device:TPU:33, one launch (start us, length us, event | category | flops | bytes accessed | tf_op | source)
XLA Modules:
  0.0 166.3 jit_solution(12527343529995544492)
XLA Ops:
  0.0 164.7 %shard_map.118 = bf16[64,1024]{1,0:T(8,128)(2,1)} custom-call(bf16[64,512]{1,0:T(8,128)(2,1)} %q_ref.1, bf16[1,2048,128]{2,1,0:T(8,128)(2,1)} %k_hbm.1, bf16[1,2048,128]{2,1,0:T(8,128)(2,1)} %v_hbm.1, bf16[512,128]{1,0:T(8,128)(2,1)} %ow_hbm.1, bf16[64,4096]{1,0:T(8,128)(2,1)} %res_hbm.1, f32[1,4096]{1,0:T(1,128)} %bitcast.8, s32[2,64]{1,0:T(2,128)} %bitcast.9, ...), custom_call_target="tpu_custom_call" | custom-call | tf_op jit(solution)/shard_map/pallas_call | solution.py:834
  164.8 1.6 copy.14

commit v5 on v4

--- a/solution.py
+++ b/solution.py
@@ -171,12 +171,14 @@
     def lanes(h):
         return pl.ds(pl.multiple_of(h * half_width, half_width), half_width)
 
-    def ring_p(t, b):
-        sems = rs_s.at[t, b], rs_r.at[t, b]
-        return send(pos.at[half - t - 1, b], posr.at[t, b], *sems, ring_next)
+    def ring_p(t, b, g):
+        sems = rs_s.at[t, 2 * b + g], rs_r.at[t, 2 * b + g]
+        cols = pl.ds(g * half_width, half_width)
+        src = pos.at[half - t - 1, b, :, cols]
+        return send(src, posr.at[t, b, :, cols], *sems, ring_next)
 
     def ring_z(t, h):
-        sems = rs_s.at[t, 2 + h], rs_r.at[t, 2 + h]
+        sems = rs_s.at[t, 4 + h], rs_r.at[t, 4 + h]
         src = dbuf.at[half - t - 1, quarter_at(2), :, lanes(h)]
         return send(src, zsr.at[t, h], *sems, ring_next)
 
@@ -403,7 +405,6 @@
         rows[z, j] = own[j] + oth[j]
         ring2(1, j, z).start()
 
-    add_second(half - 2)
     far = unit_at(half)
     for k in range(2, 4):
         pair1(half, sub_at(k), far).wait_recv()
@@ -418,9 +419,10 @@
 
     for o in (2, 1, 3):
         spread(o).start()
+    add_first(half - 1)
+    add_second(half - 2)
     dispatch(0)
     dispatch(1)
-    add_first(half - 1)
     launch(0)
     launch(1)
     add_second(half - 1)
@@ -446,7 +448,9 @@
     grid = (2 * GCAP, cnt.shape[3])
     diagonal = lax.broadcasted_iota(jnp.int32, grid, 0) == lax.broadcasted_iota(jnp.int32, grid, 1)
     row_scale = jnp.sum(jnp.where(diagonal, by_row, 0.0), axis=0, keepdims=True)
-    cnt[z, c] = jnp.where(line == 0, lead, jnp.where(line == 1, row_scale, info))
+    scale_high = row_scale.astype(BF16).astype(F32)
+    info = jnp.where(line == 12, row_scale - scale_high, info)
+    cnt[z, c] = jnp.where(line == 0, lead, jnp.where(line == 1, scale_high, info)).astype(BF16)
     to_sibling = send(cnt.at[z, c], cnt.at[z, c], c0_s.at[0], c0_r.at[0], sibling)
     to_sibling.start()
     launch(2)
@@ -483,18 +487,20 @@
     def activate(slot, units):
         many = len(units) * unit_rows
         row = lax.broadcasted_iota(jnp.int32, (many, ffw), 0).astype(F32)
-        limit = cnt[units[0], 0, 0:1, 0:1]
+        facts = [[cnt[u, b].astype(F32) for b in range(2)] for u in units]
+        limit = facts[0][0][0:1, 0:1]
         place = row
         for i in range(1, 2 * len(units)):
             later = row >= i * GCAP
-            limit = jnp.where(later, cnt[units[i // 2], i % 2, 0:1, 0:1], limit)
+            limit = jnp.where(later, facts[i // 2][i % 2][0:1, 0:1], limit)
             place = jnp.where(later, row - i * GCAP, place)
         second = place >= limit
         wide = (many, cnt.shape[3])
         at = lax.broadcasted_iota(jnp.int32, wide, 0) - lax.broadcasted_iota(jnp.int32, wide, 1)
         factor = jnp.zeros(wide, F32)
         for i, u in enumerate(units):
-            row_scale = cnt[u, 0, 1:2, :] + cnt[u, 1, 1:2, :]
+            known = facts[i][0] + facts[i][1]
+            row_scale = known[1:2] + known[12:13]
             factor = factor + jnp.where(at == i * unit_rows, row_scale, 0.0)
         factor = jnp.sum(factor, axis=1, keepdims=True)
         for e in range(2):
@@ -532,7 +538,7 @@
         for o in (1, 3):
             (over_far(o) if last else over(s, o, xin.at[s, 0])).wait_recv()
         u = unit_at(s)
-        facts = cnt[u, 0] + cnt[u, 1]
+        facts = cnt[u, 0].astype(F32) + cnt[u, 1].astype(F32)
         row = lax.broadcasted_iota(jnp.int32, (unit_rows, cnt.shape[3]), 0).astype(F32) + 1.0
         highs, lows = [], []
         for i in range(3):
@@ -556,11 +562,14 @@
             pos[s - 1, b] = total[b * block : (b + 1) * block].astype(BF16)
 
     def sum_p(t, b, arrived):
-        if arrived:
-            ring_p(t - 1, b).wait_recv()
-            at = half - t - 1
-            pos[at, b] = (pos[at, b].astype(F32) + posr[t - 1, b].astype(F32)).astype(BF16)
-        ring_p(t, b).start()
+        at = half - t - 1
+        for g in range(2):
+            if arrived:
+                ring_p(t - 1, b, g).wait_recv()
+                cols = slice(g * half_width, (g + 1) * half_width)
+                total = pos[at, b, :, cols].astype(F32) + posr[t - 1, b, :, cols].astype(F32)
+                pos[at, b, :, cols] = total.astype(BF16)
+            ring_p(t, b, g).start()
 
     def sum_z(t, h, arrived):
         if arrived:
@@ -648,13 +657,13 @@
     for o in (1, 3, 2, 0):
         down(half % 3, quarter_at(o), single)
         give(half, quarter_at(o), far).start()
+    for o in (1, 3, 2, 0):
+        down((half - 2) % 3, quarter_at(o), both(half - 2))
+        give(half - 2, quarter_at(o), unit_at(2 - half)).start()
     prepare(half, True)
     sum_z(0, c, False)
     gather_positions(half - 1)
     sum_p(1, 1 - c, False)
-    for o in (1, 3, 2, 0):
-        down((half - 2) % 3, quarter_at(o), both(half - 2))
-        give(half - 2, quarter_at(o), unit_at(2 - half)).start()
     prepare(half - 2)
     sum_z(2, 1 - c, True)
     gather_positions(half, True)
@@ -702,10 +711,12 @@
     cross(0)
     cross(1)
     sum_p(half - 1, c, True)
-    ring_p(half - 1, 1 - c).wait_recv()
+    for g in range(2):
+        ring_p(half - 1, 1 - c, g).wait_recv()
     finp[...] = (base[1 - c] + posr[half - 1, 1 - c].astype(F32)).astype(BF16)
     swap_p.start()
-    ring_p(half - 1, c).wait_recv()
+    for g in range(2):
+        ring_p(half - 1, c, g).wait_recv()
     swap_p.wait_recv()
     base[c] = base[c] + posr[half - 1, c].astype(F32) + finpr[...].astype(F32)
     for h in range(2):
@@ -739,8 +750,9 @@
                 over(s, o, xin.at[s, 0]).wait_send()
             count_pair(s, z).wait_send()
             for b in range(2):
-                ring_p(s, b).wait_send()
                 ring_z(s, b).wait_send()
+                for g in range(2):
+                    ring_p(s, b, g).wait_send()
 
         return carry
 
@@ -759,7 +771,8 @@
         send(own.at[j], oth.at[j], ot_s.at[j], ot_r.at[j], sibling).wait_send()
     for o in (1, 2, 3):
         spread(o).wait_send()
-    ring_p(0, c).wait_send()
+    for g in range(2):
+        ring_p(0, c, g).wait_send()
     ring_z(0, c).wait_send()
     swap_p.wait_send()
 
@@ -798,7 +811,7 @@
         sub,
         sub,
         pltpu.VMEM((nz, SUBS, unit_rows, width), BF16),
-        pltpu.VMEM((nz, 2, 16, 128), F32),
+        pltpu.VMEM((nz, 2, 16, 128), BF16),
         pltpu.VMEM((4, 2 * unit_rows, ffw), F32),
         pltpu.VMEM((3, 2, 2 * unit_rows, ffw), BF16),
         pltpu.VMEM((nz, SUBS, unit_rows, width), BF16),
@@ -826,7 +839,7 @@
         *[dma((half + 1,))] * 4,
         *[dma((half, SUBS))] * 2,
         *[dma((half + 1, 2))] * 2,
-        *[dma((half, SUBS))] * 2,
+        *[dma((half, 6))] * 2,
         *[dma((3,))] * 2,
         *[dma((2,))] * 2,
         *[dma((3,))] * 2,

time: 166 us -> 164 us (0.988)
  Pallas kernels: 165 us -> 162 us
    pallas_call x1, Pallas kernels: 165 us -> 162 us  [per_device(): pl.pallas_call(functools.partial(layer_kernel, nz), out_shape=jax.ShapeDt...]
where the time goes in v5:
time: 164 us
  Pallas kernels  162 us (99%)
    pallas_call x1, Pallas kernels, per_device(): pl.pallas_call(functools.partial(layer_kernel, nz), out_shape=jax.ShapeDt...  162 us

profile of v5, /device:TPU:33, one launch (start us, length us, event | category | flops | bytes accessed | tf_op | source)
XLA Modules:
  0.0 163.7 jit_solution(2594359685139404580)
XLA Ops:
  0.0 162.1 %shard_map.118 = bf16[64,1024]{1,0:T(8,128)(2,1)} custom-call(bf16[64,512]{1,0:T(8,128)(2,1)} %q_ref.1, bf16[1,2048,128]{2,1,0:T(8,128)(2,1)} %k_hbm.1, bf16[1,2048,128]{2,1,0:T(8,128)(2,1)} %v_hbm.1, bf16[512,128]{1,0:T(8,128)(2,1)} %ow_hbm.1, bf16[64,4096]{1,0:T(8,128)(2,1)} %res_hbm.1, f32[1,4096]{1,0:T(1,128)} %bitcast.8, s32[2,64]{1,0:T(2,128)} %bitcast.9, ...), custom_call_target="tpu_custom_call" | custom-call | tf_op jit(solution)/shard_map/pallas_call | solution.py:847
  162.1 1.6 copy.14

commit v6 on v5

--- a/solution.py
+++ b/solution.py
@@ -715,19 +715,6 @@
         ring_p(half - 1, 1 - c, g).wait_recv()
     finp[...] = (base[1 - c] + posr[half - 1, 1 - c].astype(F32)).astype(BF16)
     swap_p.start()
-    for g in range(2):
-        ring_p(half - 1, c, g).wait_recv()
-    swap_p.wait_recv()
-    base[c] = base[c] + posr[half - 1, c].astype(F32) + finpr[...].astype(F32)
-    for h in range(2):
-        deliver(h).wait_recv()
-        for i in range(half_width // min(unit, half_width)):
-            step = min(unit, half_width)
-            at = h * half_width + i * step
-            state = hst[x * per_sub + at // unit][:, at % unit : at % unit + step]
-            total = state.astype(F32) + base[c, :, at : at + step]
-            total = total + conr[h, :, i * step : (i + 1) * step].astype(F32)
-            out_ref[:, at : at + step] = total.astype(BF16)
     for i in range(2):
         send(ow.at[z, i], ow.at[z, i], d0_s.at[i], d0_r.at[i], sibling).wait_send()
     to_sibling.wait_send()
@@ -775,6 +762,20 @@
         ring_p(0, c, g).wait_send()
     ring_z(0, c).wait_send()
     swap_p.wait_send()
+
+    for g in range(2):
+        ring_p(half - 1, c, g).wait_recv()
+    swap_p.wait_recv()
+    base[c] = base[c] + posr[half - 1, c].astype(F32) + finpr[...].astype(F32)
+    for h in range(2):
+        deliver(h).wait_recv()
+        for i in range(half_width // min(unit, half_width)):
+            step = min(unit, half_width)
+            at = h * half_width + i * step
+            state = hst[x * per_sub + at // unit][:, at % unit : at % unit + step]
+            total = state.astype(F32) + base[c, :, at : at + step]
+            total = total + conr[h, :, i * step : (i + 1) * step].astype(F32)
+            out_ref[:, at : at + step] = total.astype(BF16)
 
 
 def per_device(nz, *args):

time: 164 us -> 163 us (level)
  no operation moved by 1% of the time
where the time goes in v6:
time: 163 us
  Pallas kernels  162 us (99%)
    pallas_call x1, Pallas kernels, per_device(): pl.pallas_call(functools.partial(layer_kernel, nz), out_shape=jax.ShapeDt...  162 us

profile of v6, /device:TPU:33, one launch (start us, length us, event | category | flops | bytes accessed | tf_op | source)
XLA Modules:
  0.0 163.2 jit_solution(1659711839401318545)
XLA Ops:
  0.0 161.6 %shard_map.118 = bf16[64,1024]{1,0:T(8,128)(2,1)} custom-call(bf16[64,512]{1,0:T(8,128)(2,1)} %q_ref.1, bf16[1,2048,128]{2,1,0:T(8,128)(2,1)} %k_hbm.1, bf16[1,2048,128]{2,1,0:T(8,128)(2,1)} %v_hbm.1, bf16[512,128]{1,0:T(8,128)(2,1)} %ow_hbm.1, bf16[64,4096]{1,0:T(8,128)(2,1)} %res_hbm.1, f32[1,4096]{1,0:T(1,128)} %bitcast.8, s32[2,64]{1,0:T(2,128)} %bitcast.9, ...), custom_call_target="tpu_custom_call" | custom-call | tf_op jit(solution)/shard_map/pallas_call | solution.py:848
  161.6 1.6 copy.14
